TPU v7x, 256 devices: a whole 4x4x8 slice. The times are simulated.
256 devices in a mesh: dp: 32 (over z, y), mp: 8 (over x, core).
Axes of the slice: x: 4, y: 4, z: 8, core: 2. Of those that a mesh axis runs over, the one named last changes fastest.
Arguments:
- features: bfloat16 [3, 512, 65536], P(None, 'mp', 'dp'), may hold values from -6 to 6
- weights: bfloat16 [11, 512, 512], P(None, 'mp'), may hold values from -0.25 to 0.25
- sample_owner: int32 [3, 65536, 1], P(None, 'dp'), may hold values from 0 to 31; in each aligned block of 2048 rows (0 to 2047, 2048 to 4095, ..., all dimensions but the last counted through in order) at most 128 rows name the same one
- sample_row: int32 [3, 65536], P(None, 'dp'), may hold values from 0 to 2047
- edge_src: int32 [8, 65536], P(None, 'dp'), may hold values from 0 to 2047
- edge_dst: int32 [8, 65536], P(None, 'dp'), may hold values from 0 to 127
- edge_count: int32 [8, 32], P(None, 'dp'), may hold values from 128 to 2048
Outputs:
- updated: bfloat16 [3, 512, 4096], P(None, 'mp', 'dp')
Inputs may be any that keep to these rules, and one draw needn't show every extreme that they name: `sample_owner`: among the 2048 entries of one node type in one block no owner appears more than 128 times; some owner appears exactly 128 times in some blocks.
All inputs are finite; a program needn't handle non-finite values.
Results may differ from a plain program's by a relative error of at most 0.0064.
Values may be sent and summed in bfloat16 or wider, within the bound.
A program may use at most 64 MiB of HBM per device.

v0:
```python
import math

import jax
import jax.numpy as jnp
from jax import lax
from jax.sharding import PartitionSpec as P

RELS = 8
SEEDS = 128


RELATION_SOURCE = (0, 1, 0, 1, 2, 0, 2, 1)
MATRIX_TARGET = (1, 0, 0, 2, 1, 2, 0, 1, 0, 1, 2)


def in_blocks(array, dim, size):
    before, after = (array.shape[:dim], array.shape[dim + 1 :])
    return jnp.moveaxis(array.reshape(*before, size, -1, *after), dim, 0)


def summed_on_arrival(array, axis, dim):
    size = lax.axis_size(axis)
    parts = lax.all_to_all(in_blocks(array, dim, size), axis, 0, 0, tiled=True)
    return jnp.sum(parts.astype(jnp.float32), axis=0)


def pick_columns(table, index):
    count = index.shape[0]
    block_size = math.gcd(count, 512)
    row_ids = jnp.arange(table.shape[1], dtype=jnp.int32)[:, None]

    def one_block(block):
        chosen = (row_ids == block[None, :]).astype(jnp.bfloat16)
        return jnp.dot(table, chosen, preferred_element_type=jnp.float32).astype(jnp.bfloat16)

    picked = lax.map(one_block, index.reshape(count // block_size, block_size))
    return picked.transpose(1, 0, 2).reshape(table.shape[0], count)


def serve_every(features, requested):
    pieces = []
    for node_kind in range(features.shape[0]):
        picked = pick_columns(features[node_kind], requested[node_kind].reshape(-1))
        pieces.append(picked.reshape(features.shape[1], requested.shape[1], requested.shape[2]))
    return lax.all_to_all(jnp.stack(pieces), "dp", split_axis=2, concat_axis=2, tiled=True)


def contract_first(left, right):
    return lax.dot_general(
        left, right, (((0,), (0,)), ((), ())), preferred_element_type=jnp.float32
    )


def per_device(features, weights, sample_owner, sample_row, edge_src, edge_dst, edge_count):
    groups = lax.axis_size("dp")
    node_kinds = features.shape[0]
    width_here = features.shape[1]
    sampled = sample_row.shape[1]
    capacity = 2 * sampled // groups
    owners = sample_owner[:, :, 0]
    owner_hot = (owners[:, :, None] == jnp.arange(groups, dtype=jnp.int32)[None, None, :]).astype(
        jnp.float32
    )
    block_size = math.gcd(sampled, 512)
    blocks = owner_hot.reshape(node_kinds, sampled // block_size, block_size, groups)
    block_ids = jnp.arange(block_size, dtype=jnp.int32)
    lower = (block_ids[:, None] >= block_ids[None, :]).astype(jnp.float32)
    within = jnp.einsum("ij,tbjo->tbio", lower, blocks, precision=lax.Precision.HIGHEST)
    totals = jnp.sum(blocks, axis=2)
    before = jnp.cumsum(totals, axis=1) - totals
    inclusive = (within + before[:, :, None, :]).reshape(node_kinds, sampled, groups)
    slot_rank = jnp.sum((inclusive - 1.0) * owner_hot, axis=2).astype(jnp.int32)
    position = owners * capacity + slot_rank
    rank_hot = (
        slot_rank[:, :, None] == jnp.arange(capacity, dtype=jnp.int32)[None, None, :]
    ).astype(jnp.float32)
    weighted_owner = owner_hot * sample_row[:, :, None].astype(jnp.float32)
    requests = jnp.einsum(
        "tio,tik->tok", weighted_owner, rank_hot, precision=lax.Precision.HIGHEST
    ).astype(jnp.int32)
    fetched = serve_every(
        features, lax.all_to_all(requests, "dp", split_axis=1, concat_axis=1, tiled=True)
    )
    fetched = fetched.reshape(node_kinds, width_here, groups * capacity)
    gathered = jnp.stack(
        [pick_columns(fetched[node_kind], position[node_kind]) for node_kind in range(node_kinds)]
    )
    edge_total = edge_src.shape[1]
    seed_ids = jnp.arange(SEEDS, dtype=jnp.int32)[:, None]
    slot_ids = jnp.arange(edge_total, dtype=jnp.int32)
    messages = []
    for relation in range(RELS):
        live_edge = slot_ids < edge_count[relation, 0]
        target = jnp.where(live_edge, edge_dst[relation], -1)
        dst_hot = (seed_ids == target[None, :]).astype(jnp.bfloat16)
        sources = pick_columns(gathered[RELATION_SOURCE[relation]], edge_src[relation])
        summed = lax.dot_general(
            sources, dst_hot, (((1,), (1,)), ((), ())), preferred_element_type=jnp.float32
        )
        degree = jnp.sum(dst_hot, axis=1, dtype=jnp.float32)
        messages.append((summed / jnp.maximum(degree, 1.0)[None, :]).astype(jnp.bfloat16))
    for node_kind in range(node_kinds):
        messages.append(gathered[node_kind, :, :SEEDS])
    stacked = jnp.stack(messages)
    full_width = weights.shape[2]
    partial_sums = [jnp.zeros((full_width, SEEDS), jnp.float32) for node_kind in range(node_kinds)]
    for matrix in range(stacked.shape[0]):
        partial_sums[MATRIX_TARGET[matrix]] = partial_sums[MATRIX_TARGET[matrix]] + contract_first(
            weights[matrix], stacked[matrix]
        )
    typed = summed_on_arrival(jnp.stack(partial_sums).astype(jnp.bfloat16), "mp", 1)
    return jax.nn.relu(typed).astype(jnp.bfloat16)


def solution(mesh):
    return jax.shard_map(
        per_device,
        mesh=mesh,
        in_specs=(
            P(None, "mp", "dp"),
            P(None, "mp", None),
            P(None, "dp", None),
            P(None, "dp"),
            P(None, "dp"),
            P(None, "dp"),
            P(None, "dp"),
        ),
        out_specs=P(None, "mp", "dp"),
        check_vma=False,
    )
```

profile of v0, /device:TPU:1, one launch (start us, length us, event | category | flops | bytes accessed | tf_op | source)
XLA Modules:
  0.0 161.7 jit_solution(3690651321167936651)
XLA Ops:
  2.4 1.8 %fusion.110 = s32[3,32,128]{2,1,0:T(8,128)S(1)} fusion(s32[3,2048]{1,0:T(4,128)S(1)} %bitcast.386, f32[3,2048]{1,0:T(4,128)S(1)} %convert_element_type.204, s32[3,2048]{1,0:T(4,128)S(1)} %bitcast.412), kind=kOutput, calls=%fused_computation.135 | convolution fusion | flops 303181824 | bytes 122880 | tf_op jit(solution)/shard_map/tio,tik->tok/dot_general | solution.py:78
  4.9 12.0 %all-to-all-start = ((s32[3,32,128]{2,0,1:T(4,128)}), s32[3,32,128]{2,0,1:T(4,128)S(1)}, u32[]{:S(2)}, u32[]{:S(2)}) async-start(s32[3,32,128]{2,0,1:T(4,128)} %copy.80), calls=%async_computation | async-start | bytes 131072 | tf_op jit(solution)/shard_map/all_to_all | solution.py:82
  18.2 7.6 %all-to-all-done = s32[3,32,128]{2,0,1:T(4,128)S(1)} async-done(((s32[3,32,128]{2,0,1:T(4,128)}), s32[3,32,128]{2,0,1:T(4,128)S(1)}, u32[]{:S(2)}, u32[]{:S(2)}) %all-to-all-start) | async-done | bytes 49184 | tf_op jit(solution)/shard_map/all_to_all | solution.py:82
  26.0 6.6 %while.155 = (s32[]{:T(128)}, bf16[8,64,512]{2,1,0:T(8,128)(2,1)S(1)}, s32[8,512]{1,0:T(8,128)S(1)}, bf16[64,2048]{1,0:T(8,128)(2,1)S(1)}, s32[]{:T(128)}) while((s32[]{:T(128)}, bf16[8,64,512]{2,1,0:T(8,128)(2,1)S(1)}, s32[8,512]{1,0:T(8,128)S(1)}, bf16[64,2048]{1,0:T(8,128)(2,1)S(1)}, s32[]{:T(128)}) %tuple.261), condition=%wide.region_6.7_spmd.clone, body=%wide.region_5.6_spmd.clone.sunk | while | flops 135299072 | bytes 333893 | solution.py:36
  33.3 6.6 %while.156 = (s32[]{:T(128)}, bf16[8,64,512]{2,1,0:T(8,128)(2,1)S(1)}, s32[8,512]{1,0:T(8,128)S(1)}, bf16[64,2048]{1,0:T(8,128)(2,1)S(1)}, s32[]{:T(128)}) while((s32[]{:T(128)}, bf16[8,64,512]{2,1,0:T(8,128)(2,1)S(1)}, s32[8,512]{1,0:T(8,128)S(1)}, bf16[64,2048]{1,0:T(8,128)(2,1)S(1)}, s32[]{:T(128)}) %tuple.258), condition=%wide.region_8.9_spmd.clone, body=%wide.region_7.8_spmd.clone.sunk | while | flops 135299072 | bytes 333893 | solution.py:36
  40.6 6.6 %while.154 = (s32[]{:T(128)}, bf16[8,64,512]{2,1,0:T(8,128)(2,1)S(1)}, s32[8,512]{1,0:T(8,128)S(1)}, bf16[64,2048]{1,0:T(8,128)(2,1)S(1)}, s32[]{:T(128)}) while((s32[]{:T(128)}, bf16[8,64,512]{2,1,0:T(8,128)(2,1)S(1)}, s32[8,512]{1,0:T(8,128)S(1)}, bf16[64,2048]{1,0:T(8,128)(2,1)S(1)}, s32[]{:T(128)}) %tuple.264), condition=%wide.region_4.5_spmd.clone, body=%wide.region_3.4_spmd.clone.sunk | while | flops 135299072 | bytes 333893 | solution.py:36
  48.1 1.8 %copy.84 = bf16[3,64,32,128]{3,1,0,2:T(8,128)(2,1)} copy(bf16[3,64,32,128]{3,2,1,0:T(8,128)(2,1)S(1)} %pad_maximum_fusion) | data formatting | bytes 3145728 | tf_op jit(solution)/shard_map/stack | solution.py:45
  49.9 4.3 %all-to-all-start.1 = ((bf16[3,64,32,128]{3,1,0,2:T(8,128)(2,1)}), bf16[3,64,32,128]{3,1,0,2:T(8,128)(2,1)S(1)}, u32[]{:S(2)}, u32[]{:S(2)}) async-start(bf16[3,64,32,128]{3,1,0,2:T(8,128)(2,1)} %copy.84), calls=%async_computation.1 | async-start | bytes 3145728 | tf_op jit(solution)/shard_map/all_to_all | solution.py:45
  54.2 5.1 %compare_select_fusion.5 = (s32[1,2048]{1,0:T(1,128)S(1)}, s32[1,2048]{1,0:T(1,128)S(1)}, s32[1,2048]{1,0:T(1,128)S(1)}, s32[1,2048]{1,0:T(1,128)S(1)}, s32[1,20...) fusion(s32[8,2048]{1,0:T(8,128)S(1)} %copy-done.6, s32[]{:T(128)} %bitcast.21, ...), kind=kLoop, calls=%fused_computation.235 | loop fusion | flops 32768 | bytes 131104 | tf_op jit(solution)/shard_map/jit(_where)/select_n | solution.py:94
  63.0 26.3 %all-to-all-done.1 = bf16[3,64,32,128]{3,1,0,2:T(8,128)(2,1)S(1)} async-done(((bf16[3,64,32,128]{3,1,0,2:T(8,128)(2,1)}), bf16[3,64,32,128]{3,1,0,2:T(8,128)(2,1)S(1)}, u32[]{:S(2)}, u32[]{:S(2)}) %all-to-all-start.1) | async-done | bytes 1572896 | tf_op jit(solution)/shard_map/all_to_all | solution.py:45
  90.0 5.9 %while.157 = (s32[]{:T(128)}, bf16[4,64,512]{2,1,0:T(8,128)(2,1)S(1)}, s32[4,512]{1,0:T(4,128)S(1)}, bf16[64,4096]{1,0:T(8,128)(2,1)S(1)}, s32[]{:T(128)}) while((s32[]{:T(128)}, bf16[4,64,512]{2,1,0:T(8,128)(2,1)S(1)}, s32[4,512]{1,0:T(4,128)S(1)}, bf16[64,4096]{1,0:T(8,128)(2,1)S(1)}, s32[]{:T(128)}) %tuple.300), condition=%wide.region_10.11_spmd.clone, body=%wide.region_9.10_spmd.clone.sunk | while | flops 270565376 | bytes 596037 | solution.py:36
  91.5 1.4 fusion.243
  94.5 1.4 fusion.243
  96.0 3.3 %while.158 = (s32[]{:T(128)}, bf16[4,64,512]{2,1,0:T(8,128)(2,1)S(1)}, s32[4,512]{1,0:T(4,128)S(1)}, bf16[64,2048]{1,0:T(8,128)(2,1)S(1)}, s32[]{:T(128)}) while((s32[]{:T(128)}, bf16[4,64,512]{2,1,0:T(8,128)(2,1)S(1)}, s32[4,512]{1,0:T(4,128)S(1)}, bf16[64,2048]{1,0:T(8,128)(2,1)S(1)}, s32[]{:T(128)}) %tuple.303), condition=%wide.region_12.13_spmd.clone, body=%wide.region_11.12_spmd.clone.sunk | while | flops 135299072 | bytes 333893 | solution.py:36
  100.0 5.9 %while.159 = (s32[]{:T(128)}, bf16[4,64,512]{2,1,0:T(8,128)(2,1)S(1)}, s32[4,512]{1,0:T(4,128)S(1)}, bf16[64,4096]{1,0:T(8,128)(2,1)S(1)}, s32[]{:T(128)}) while((s32[]{:T(128)}, bf16[4,64,512]{2,1,0:T(8,128)(2,1)S(1)}, s32[4,512]{1,0:T(4,128)S(1)}, bf16[64,4096]{1,0:T(8,128)(2,1)S(1)}, s32[]{:T(128)}) %tuple.301), condition=%wide.region_15.16_spmd.clone, body=%wide.region_14.15_spmd.clone.sunk | while | flops 270565376 | bytes 596037 | solution.py:36
  106.0 3.3 %while.160 = (s32[]{:T(128)}, bf16[4,64,512]{2,1,0:T(8,128)(2,1)S(1)}, s32[4,512]{1,0:T(4,128)S(1)}, bf16[64,2048]{1,0:T(8,128)(2,1)S(1)}, s32[]{:T(128)}) while((s32[]{:T(128)}, bf16[4,64,512]{2,1,0:T(8,128)(2,1)S(1)}, s32[4,512]{1,0:T(4,128)S(1)}, bf16[64,2048]{1,0:T(8,128)(2,1)S(1)}, s32[]{:T(128)}) %tuple.306), condition=%wide.region_17.18_spmd.clone, body=%wide.region_16.17_spmd.clone.sunk | while | flops 135299072 | bytes 333893 | solution.py:36
  109.9 5.9 %while.161 = (s32[]{:T(128)}, bf16[4,64,512]{2,1,0:T(8,128)(2,1)S(1)}, s32[4,512]{1,0:T(4,128)S(1)}, bf16[64,4096]{1,0:T(8,128)(2,1)S(1)}, s32[]{:T(128)}) while((s32[]{:T(128)}, bf16[4,64,512]{2,1,0:T(8,128)(2,1)S(1)}, s32[4,512]{1,0:T(4,128)S(1)}, bf16[64,4096]{1,0:T(8,128)(2,1)S(1)}, s32[]{:T(128)}) %tuple.302), condition=%wide.region_20.21_spmd.clone, body=%wide.region_19.20_spmd.clone.sunk | while | flops 270565376 | bytes 596037 | solution.py:36
  115.9 3.3 %while.162 = (s32[]{:T(128)}, bf16[4,64,512]{2,1,0:T(8,128)(2,1)S(1)}, s32[4,512]{1,0:T(4,128)S(1)}, bf16[64,2048]{1,0:T(8,128)(2,1)S(1)}, s32[]{:T(128)}) while((s32[]{:T(128)}, bf16[4,64,512]{2,1,0:T(8,128)(2,1)S(1)}, s32[4,512]{1,0:T(4,128)S(1)}, bf16[64,2048]{1,0:T(8,128)(2,1)S(1)}, s32[]{:T(128)}) %tuple.309), condition=%wide.region_22.23_spmd.clone, body=%wide.region_21.22_spmd.clone.sunk | while | flops 135299072 | bytes 333893 | solution.py:36
  122.6 3.5 %while.163 = (s32[]{:T(128)}, bf16[4,64,512]{2,1,0:T(8,128)(2,1)S(1)}, s32[4,512]{1,0:T(4,128)S(1)}, bf16[64,2048]{1,0:T(8,128)(2,1)S(1)}, s32[]{:T(128)}) while((s32[]{:T(128)}, bf16[4,64,512]{2,1,0:T(8,128)(2,1)S(1)}, s32[4,512]{1,0:T(4,128)S(1)}, bf16[64,2048]{1,0:T(8,128)(2,1)S(1)}, s32[]{:T(128)}) %tuple.307), condition=%wide.region_25.26_spmd.clone, body=%wide.region_24.25_spmd.clone.sunk | while | flops 135299072 | bytes 333893 | solution.py:36
  126.2 3.3 %while.164 = (s32[]{:T(128)}, bf16[4,64,512]{2,1,0:T(8,128)(2,1)S(1)}, s32[4,512]{1,0:T(4,128)S(1)}, bf16[64,2048]{1,0:T(8,128)(2,1)S(1)}, s32[]{:T(128)}) while((s32[]{:T(128)}, bf16[4,64,512]{2,1,0:T(8,128)(2,1)S(1)}, s32[4,512]{1,0:T(4,128)S(1)}, bf16[64,2048]{1,0:T(8,128)(2,1)S(1)}, s32[]{:T(128)}) %tuple.310), condition=%wide.region_28.29_spmd.clone, body=%wide.region_27.28_spmd.clone.sunk | while | flops 135299072 | bytes 333893 | solution.py:36
  129.6 3.3 %while.165 = (s32[]{:T(128)}, bf16[4,64,512]{2,1,0:T(8,128)(2,1)S(1)}, s32[4,512]{1,0:T(4,128)S(1)}, bf16[64,2048]{1,0:T(8,128)(2,1)S(1)}, s32[]{:T(128)}) while((s32[]{:T(128)}, bf16[4,64,512]{2,1,0:T(8,128)(2,1)S(1)}, s32[4,512]{1,0:T(4,128)S(1)}, bf16[64,2048]{1,0:T(8,128)(2,1)S(1)}, s32[]{:T(128)}) %tuple.304), condition=%wide.region_31.32_spmd.clone, body=%wide.region_30.31_spmd.clone.sunk | while | flops 135299072 | bytes 333893 | solution.py:36
  135.7 3.3 %while.166 = (s32[]{:T(128)}, bf16[4,64,512]{2,1,0:T(8,128)(2,1)S(1)}, s32[4,512]{1,0:T(4,128)S(1)}, bf16[64,2048]{1,0:T(8,128)(2,1)S(1)}, s32[]{:T(128)}) while((s32[]{:T(128)}, bf16[4,64,512]{2,1,0:T(8,128)(2,1)S(1)}, s32[4,512]{1,0:T(4,128)S(1)}, bf16[64,2048]{1,0:T(8,128)(2,1)S(1)}, s32[]{:T(128)}) %tuple.305), condition=%wide.region_34.35_spmd.clone, body=%wide.region_33.34_spmd.clone.sunk | while | flops 135299072 | bytes 333893 | solution.py:36
  139.1 3.3 %while.167 = (s32[]{:T(128)}, bf16[4,64,512]{2,1,0:T(8,128)(2,1)S(1)}, s32[4,512]{1,0:T(4,128)S(1)}, bf16[64,2048]{1,0:T(8,128)(2,1)S(1)}, s32[]{:T(128)}) while((s32[]{:T(128)}, bf16[4,64,512]{2,1,0:T(8,128)(2,1)S(1)}, s32[4,512]{1,0:T(4,128)S(1)}, bf16[64,2048]{1,0:T(8,128)(2,1)S(1)}, s32[]{:T(128)}) %tuple.308), condition=%wide.region_37.38_spmd.clone, body=%wide.region_36.37_spmd.clone.sunk | while | flops 135299072 | bytes 333893 | solution.py:36
  144.6 16.4 %all_to_all.15 = bf16[8,3,64,128]{3,2,1,0:T(8,128)(2,1)S(1)} all-to-all(bf16[8,3,64,128]{3,2,1,0:T(8,128)(2,1)S(1)} %copy.105), channel_id=1, replica_groups=mesh['dp'=32,'mp'=8] {'mp'}, dimensions={0} | all-to-all | bytes 786432 | tf_op jit(solution)/shard_map/all_to_all | solution.py:23
  (270 shorter events, 80.4 us)
Async XLA Ops:
  0.0 2.4 %copy-start.7 = (s32[3,2048]{1,0:T(4,128)S(1)}, s32[3,2048]{1,0:T(4,128)}, u32[]{:S(2)}) copy-start(s32[3,2048]{1,0:T(4,128)} %param.38) | copy-start | bytes 73732
  2.3 14.6 %copy-start.4 = (s32[3,2048,1]{1,2,0:T(1,128)S(1)}, s32[3,2048,1]{1,2,0:T(1,128)}, u32[]{:S(2)}) copy-start(s32[3,2048,1]{1,2,0:T(1,128)} %param.37) | copy-start | bytes 73732
  2.3 14.7 %copy-start = (bf16[3,64,2048]{2,1,0:T(8,128)(2,1)S(1)}, bf16[3,64,2048]{2,1,0:T(8,128)(2,1)}, u32[]{:S(2)}) copy-start(bf16[3,64,2048]{2,1,0:T(8,128)(2,1)} %param.35) | copy-start | bytes 2359300
  2.4 14.8 %copy-start.5 = (s32[8,2048]{1,0:T(8,128)S(1)}, s32[8,2048]{1,0:T(8,128)}, u32[]{:S(2)}) copy-start(s32[8,2048]{1,0:T(8,128)} %param.39) | copy-start | bytes 196612
  4.3 13.2 %copy-start.8 = (s32[8,1]{0,1:T(1,128)S(1)}, s32[8,1]{0,1:T(1,128)}, u32[]{:S(2)}) copy-start(s32[8,1]{0,1:T(1,128)} %param.41) | copy-start | bytes 100
  4.9 20.9 %all-to-all-start = ((s32[3,32,128]{2,0,1:T(4,128)}), s32[3,32,128]{2,0,1:T(4,128)S(1)}, u32[]{:S(2)}, u32[]{:S(2)}) async-start(s32[3,32,128]{2,0,1:T(4,128)} %copy.80), calls=%async_computation | async-start | bytes 131072 | tf_op jit(solution)/shard_map/all_to_all | solution.py:82
  49.9 4.3 %copy-start.6 = (s32[8,2048]{1,0:T(8,128)S(1)}, s32[8,2048]{1,0:T(8,128)}, u32[]{:S(2)}) copy-start(s32[8,2048]{1,0:T(8,128)} %param.40) | copy-start | bytes 196612
  49.9 39.4 %all-to-all-start.1 = ((bf16[3,64,32,128]{3,1,0,2:T(8,128)(2,1)}), bf16[3,64,32,128]{3,1,0,2:T(8,128)(2,1)S(1)}, u32[]{:S(2)}, u32[]{:S(2)}) async-start(bf16[3,64,32,128]{3,1,0,2:T(8,128)(2,1)} %copy.84), calls=%async_computation.1 | async-start | bytes 3145728 | tf_op jit(solution)/shard_map/all_to_all | solution.py:45
  119.3 0.7 copy-start.2
  119.3 1.2 copy-start.1
  119.3 1.2 copy-start.12
  119.3 1.8 %copy-start.9 = (f32[128]{0:T(128)S(1)}, f32[128]{0:T(128)}, u32[]{:S(2)}) copy-start(f32[128]{0:T(128)} %broadcast_maximum_fusion.6) | copy-start | bytes 1540
  122.6 3.6 %copy-start.3 = (bf16[64,2048]{1,0:T(8,128)(2,1)S(1)}, bf16[64,2048]{1,0:T(8,128)(2,1)}, u32[]{:S(2)}) copy-start(bf16[64,2048]{1,0:T(8,128)(2,1)} %copy-done.2) | copy-start | bytes 786436
  132.9 0.6 copy-start.11
  142.4 0.7 copy-start.10
where the time goes:
time: 162 us
  matrix products  69.4 us (43%)
  waiting for transfers between devices  33.9 us (21%)
  blocking collectives  16.4 us (10%)
  starting transfers between devices  16.3 us (10%)
  local copies, waits for them, and re-layouts  11.9 us (7%)
  other arithmetic  10.7 us (7%)
  loops' own time  2.21 us (1%)
    dot_general x68, matrix products, one_block(): jnp.dot(table, chosen, preferred_element_type=jnp.float32)  61.8 us
    all_to_all x1, waiting for transfers between devices, serve_every(): lax.all_to_all(jnp.stack(pieces), 'dp', split_axis=2, concat_axis=2, tile...  26.3 us
    all_to_all x1, blocking collectives, summed_on_arrival(): parts = lax.all_to_all(in_blocks(array, dim, size), axis, 0, 0, tiled=True)  16.4 us
    all_to_all x1, starting transfers between devices, per_device(): lax.all_to_all(requests, 'dp', split_axis=1, concat_axis=1, tiled=True)  12 us
    all_to_all x1, waiting for transfers between devices, per_device(): lax.all_to_all(requests, 'dp', split_axis=1, concat_axis=1, tiled=True)  7.6 us
    dot_general x11, matrix products, contract_first(): lax.dot_general(left, right, (((0,), (0,)), ((), ())), preferred_element_...  5.2 us
    select_n x1, other arithmetic, per_device(): target = jnp.where(live_edge, edge_dst[relation], -1)  5.12 us
    all_to_all x1, starting transfers between devices, serve_every(): lax.all_to_all(jnp.stack(pieces), 'dp', split_axis=2, concat_axis=2, tile...  4.28 us
  transfers between devices with their start and end apart: 2, of which 2 were waited for; matrix products, arithmetic and copies ran while one was open for 6% of the time, Pallas kernels for 0%

commit v1 on v0

v1 whole, which is shorter than its diff:
```python
import functools

import jax
import jax.numpy as jnp
from jax import lax
from jax.experimental import pallas as pl
from jax.experimental.pallas import tpu as pltpu
from jax.sharding import PartitionSpec as P

TYPES = 3
RELS = 8
SEEDS = 128
CAP = 128
RELATION_SOURCE = (0, 1, 0, 1, 2, 0, 2, 1)
STACKS = ((1, 2, 6, 8), (0, 4, 7, 9), (3, 5, 10))
NZ, NY = 8, 4
DP = NZ * NY
MESH = pl.DeviceIdType.MESH
F32, BF16, I32 = jnp.float32, jnp.bfloat16, jnp.int32
EB = 512


def iota(shape, dim):
    return lax.broadcasted_iota(I32, shape, dim)


def hot(ids, rows):
    return (iota((rows, ids.shape[1]), 0) == ids).astype(F32).astype(BF16)


def dot(a, b):
    return jnp.dot(a, b, preferred_element_type=F32)


def dot_nt(a, b):
    return lax.dot_general(a, b, (((1,), (1,)), ((), ())), preferred_element_type=F32)


def kernel(n_mp, feat, w, own, row, esrc, edst, ecnt, out, rq, req_out, req_in, send, recv,
           lk, pc, plo, msgs, wt, psend, precv, rs, rr, ss, sr, ps, pr):
    me, mm = lax.axis_index("dp"), lax.axis_index("mp")
    z, y = me // NY, me % NY

    def fwd(s):
        return ((z + s // NY) % NZ) * NY + (y + s % NY) % NY

    def bwd(s):
        return ((z + NZ - s // NY) % NZ) * NY + (y + NY - s % NY) % NY

    barrier = pltpu.get_barrier_semaphore()

    def greet(s, _):
        pl.semaphore_signal(barrier, 1, device_id={"dp": fwd(s)}, device_id_type=MESH)
        return 0

    lax.fori_loop(1, DP, greet, 0)

    def greet_mp(d, _):
        pl.semaphore_signal(barrier, 1, device_id={"mp": (mm + d) % n_mp}, device_id_type=MESH)
        return 0

    lax.fori_loop(1, n_mp, greet_mp, 0)

    upper = (iota((256, 256), 0) <= iota((256, 256), 1)).astype(F32).astype(BF16)
    base = jnp.zeros((TYPES * DP, 1), F32)
    acc = [jnp.zeros((2 * DP, CAP), F32) for _ in range(TYPES)]
    for blk in range(8):
        lanes = slice(blk * 256, (blk + 1) * 256)
        owners = [own[t, :, lanes] for t in range(TYPES)]
        ohs = [(iota((DP, 256), 0) == owners[t]).astype(F32) for t in range(TYPES)]
        oh = jnp.concatenate(ohs, axis=0)
        incl = dot(oh.astype(BF16), upper) + base
        base = incl[:, 255:256]
        ranked = oh * (incl - 1.0)
        for t in range(TYPES):
            rank = jnp.sum(ranked[t * DP:(t + 1) * DP], axis=0, keepdims=True).astype(I32)
            ids = row[t:t + 1, lanes]
            left = jnp.concatenate(
                [ohs[t] * (ids >> 8).astype(F32), ohs[t] * (ids & 255).astype(F32)], axis=0
            ).astype(BF16)
            acc[t] = acc[t] + dot_nt(left, hot(rank, CAP))
            lk[t, blk:blk + 1, :] = (owners[t] >> 1).astype(F32)
            lk[t, 8 + blk:9 + blk, :] = ((owners[t] & 1) * CAP + rank).astype(F32)
    for t in range(TYPES):
        rq[t * DP:(t + 1) * DP, :] = (acc[t][:DP] * 256.0 + acc[t][DP:]).astype(I32)
    for o in range(DP):
        req_out[o, :, :] = rq[pl.ds(o, TYPES, stride=DP), :]

    pl.semaphore_wait(barrier, DP - 1 + n_mp - 1)

    def req_copy(s):
        return pltpu.make_async_remote_copy(
            req_out.at[fwd(s)], req_in.at[me], rs.at[s], rr.at[s],
            device_id={"dp": fwd(s)}, device_id_type=MESH)

    def ask(s, _):
        req_copy(s).start()
        return 0

    lax.fori_loop(1, DP, ask, 0)
    req_in[me] = req_out[me]

    def row_copy(t, s):
        return pltpu.make_async_remote_copy(
            send.at[t, bwd(s)], recv.at[t, me], ss.at[t, s], sr.at[t, s],
            device_id={"dp": bwd(s)}, device_id_type=MESH)

    def serve(t, dz, first):
        peers = [bwd(dz * NY + j) for j in range(NY)]
        if t == 0:
            for j in range(NY):
                if not (first and j == 0):
                    req_copy(dz * NY + j).wait_recv()
        ids = jnp.concatenate([req_in[peers[j], t:t + 1, :] for j in range(NY)], axis=1)
        low, high = ids & 255, ids >> 8
        table = jnp.concatenate([feat[t, :, c * 256:(c + 1) * 256] for c in range(8)], axis=0)
        res = dot(table, hot(low, 256))
        picked = res[0:64]
        for c in range(1, 8):
            picked = jnp.where(high == c, res[c * 64:(c + 1) * 64], picked)
        picked = picked.astype(BF16)
        for j in range(NY):
            piece = picked[:, j * CAP:(j + 1) * CAP]
            if first and j == 0:
                recv[t, me] = piece
            else:
                send[t, peers[j]] = piece
        for j in range(NY):
            if not (first and j == 0):
                row_copy(t, dz * NY + j).start()

    def zorder(i):
        return (i % 2) * ((i + 1) // 2) + (1 - i % 2) * ((NZ - i // 2) % NZ)

    for t in range(TYPES):
        serve(t, 0, True)

        def step(i, _, t=t):
            serve(t, zorder(i), False)
            return 0

        lax.fori_loop(1, NZ, step, 0)

    for r in range(RELS):
        t = RELATION_SOURCE[r]

        def look(k, _, r=r, t=t):
            lanes = pl.ds(pl.multiple_of(k * EB, EB), EB)
            src = esrc[r:r + 1, lanes]
            res = dot(lk[t].astype(BF16), hot(src & 255, 256))
            here = iota((8, EB), 0) == (src >> 8)
            pc[r:r + 1, lanes] = jnp.sum(jnp.where(here, res[:8], 0.0), axis=0, keepdims=True)
            plo[r:r + 1, lanes] = jnp.sum(jnp.where(here, res[8:], 0.0), axis=0, keepdims=True)
            return 0

        lax.fori_loop(0, 2048 // EB, look, 0)

    for a in range(TYPES):
        mats = [w[m].astype(F32) for m in STACKS[a]]
        if len(mats) < 4:
            mats.append(jnp.zeros_like(mats[0]))
            msgs[a, 192:256, :] = jnp.zeros((64, SEEDS), BF16)
        wt[a] = jnp.concatenate(mats, axis=0).T.astype(BF16)

    def pick(t, chunk, low):
        oh = hot(low.astype(I32), 256)
        picked = None
        for g in range(4):
            left = jnp.concatenate(
                [jnp.concatenate([recv[t, 2 * c], recv[t, 2 * c + 1]], axis=1)
                 for c in range(4 * g, 4 * g + 4)], axis=0)
            res = dot(left, oh)
            for k in range(4):
                part = res[k * 64:(k + 1) * 64]
                picked = part if picked is None else jnp.where(chunk == float(4 * g + k), part, picked)
        return picked.astype(BF16)

    def place(m):
        for a in range(TYPES):
            if m in STACKS[a]:
                return a, STACKS[a].index(m) * 64

    for t in range(TYPES):
        def land(s, _, t=t):
            row_copy(t, s).wait_recv()
            return 0

        lax.fori_loop(1, DP, land, 0)
        a, k = place(RELS + t)
        msgs[a, k:k + 64, :] = pick(t, lk[t, 0:1, 0:SEEDS], lk[t, 8:9, 0:SEEDS])
        for r in range(RELS):
            if RELATION_SOURCE[r] != t:
                continue
            count = ecnt[0, r]

            def edges(k, total, r=r, t=t, count=count):
                lanes = pl.ds(pl.multiple_of(k * EB, EB), EB)
                rows = pick(t, pc[r:r + 1, lanes], plo[r:r + 1, lanes])
                rows = jnp.concatenate([rows, jnp.ones((16, EB), BF16)], axis=0)
                slot = iota((1, EB), 1) + k * EB
                target = jnp.where(slot < count, edst[r:r + 1, lanes], -1)
                return total + dot_nt(rows, hot(target, SEEDS))

            total = lax.fori_loop(0, 2048 // EB, edges, jnp.zeros((80, SEEDS), F32))
            a, k = place(r)
            msgs[a, k:k + 64, :] = (total[:64] / jnp.maximum(total[64:65], 1.0)).astype(BF16)

    def part_copy(a, d):
        return pltpu.make_async_remote_copy(
            psend.at[a, (mm + d) % n_mp], precv.at[a, mm], ps.at[a, d], pr.at[a, d],
            device_id={"mp": (mm + d) % n_mp}, device_id_type=MESH)

    for a in range(TYPES):
        part = dot(wt[a], msgs[a]).astype(BF16)
        for p in range(n_mp):
            psend[a, p] = part[p * 64:(p + 1) * 64]
        for d in range(1, n_mp):
            part_copy(a, d).start()
        precv[a, mm] = psend[a, mm]
    for a in range(TYPES):
        for d in range(1, n_mp):
            part_copy(a, d).wait_recv()
        typed = precv[a, 0].astype(F32)
        for p in range(1, n_mp):
            typed = typed + precv[a, p].astype(F32)
        out[a] = jnp.maximum(typed, 0.0).astype(BF16)

    def drain(s, _):
        req_copy(s).wait_send()
        for t in range(TYPES):
            row_copy(t, s).wait_send()
        return 0

    lax.fori_loop(1, DP, drain, 0)
    for a in range(TYPES):
        for d in range(1, n_mp):
            part_copy(a, d).wait_send()


def solution(mesh):
    n_mp = mesh.shape["mp"]

    def per_device(features, weights, sample_owner, sample_row, edge_src, edge_dst, edge_count):
        vmem = pl.BlockSpec(memory_space=pltpu.VMEM)
        return pl.pallas_call(
            functools.partial(kernel, n_mp),
            out_shape=jax.ShapeDtypeStruct((TYPES, 64, SEEDS), BF16),
            in_specs=[vmem] * 6 + [pl.BlockSpec(memory_space=pltpu.SMEM)],
            out_specs=vmem,
            scratch_shapes=[
                pltpu.VMEM((TYPES * DP, CAP), I32),
                pltpu.VMEM((DP, TYPES, CAP), I32),
                pltpu.VMEM((DP, TYPES, CAP), I32),
                pltpu.VMEM((TYPES, DP, 64, CAP), BF16),
                pltpu.VMEM((TYPES, DP, 64, CAP), BF16),
                pltpu.VMEM((TYPES, 16, 256), F32),
                pltpu.VMEM((RELS, 2048), F32),
                pltpu.VMEM((RELS, 2048), F32),
                pltpu.VMEM((TYPES, 256, SEEDS), BF16),
                pltpu.VMEM((TYPES, 512, 256), BF16),
                pltpu.VMEM((TYPES, n_mp, 64, SEEDS), BF16),
                pltpu.VMEM((TYPES, n_mp, 64, SEEDS), BF16),
                pltpu.SemaphoreType.DMA((DP,)),
                pltpu.SemaphoreType.DMA((DP,)),
                pltpu.SemaphoreType.DMA((TYPES, DP)),
                pltpu.SemaphoreType.DMA((TYPES, DP)),
                pltpu.SemaphoreType.DMA((TYPES, n_mp)),
                pltpu.SemaphoreType.DMA((TYPES, n_mp)),
            ],
            compiler_params=pltpu.CompilerParams(
                collective_id=0, has_side_effects=True, vmem_limit_bytes=56 << 20),
        )(features, weights, jnp.transpose(sample_owner, (0, 2, 1)), sample_row,
          edge_src, edge_dst, jnp.transpose(edge_count, (1, 0)))

    return jax.shard_map(
        per_device,
        mesh=mesh,
        in_specs=(
            P(None, "mp", "dp"),
            P(None, "mp", None),
            P(None, "dp", None),
            P(None, "dp"),
            P(None, "dp"),
            P(None, "dp"),
            P(None, "dp"),
        ),
        out_specs=P(None, "mp", "dp"),
        check_vma=False,
    )
```

time: 162 us -> 70.9 us (0.44)
  matrix products: 69.4 us -> 0 us
  Pallas kernels: 0 us -> 69.3 us
  waiting for transfers between devices: 33.9 us -> 0 us
  blocking collectives: 16.4 us -> 0 us
  starting transfers between devices: 16.3 us -> 0 us
  other arithmetic: 10.7 us -> 0 us
  local copies, waits for them, and re-layouts: 11.9 us -> 1.42 us
  loops' own time: 2.21 us -> 0 us
    dot_general x81 -> x0, matrix products: 69.4 us -> none  [the longest x68 61.8 us: one_block(): jnp.dot(table, chosen, preferred_element_type=jnp.float32)]
    pallas_call x0 -> x1, Pallas kernels: none -> 69.3 us  [per_device(): pl.pallas_call(functools.partial(kernel, n_mp), out_shape=jax.ShapeDtypeS...]
    all_to_all x2 -> x0, waiting for transfers between devices: 33.9 us -> none  [the longest x1 26.3 us: serve_every(): lax.all_to_all(jnp.stack(pieces), 'dp', split_axis=2, concat_axis=2, tile...]
    all_to_all x1 -> x0, blocking collectives: 16.4 us -> none  [summed_on_arrival(): parts = lax.all_to_all(in_blocks(array, dim, size), axis, 0, 0, tiled=True)]
    all_to_all x2 -> x0, starting transfers between devices: 16.3 us -> none  [the longest x1 12 us: per_device(): lax.all_to_all(requests, 'dp', split_axis=1, concat_axis=1, tiled=True)]
    select_n x1 -> x0, other arithmetic: 5.12 us -> none  [per_device(): target = jnp.where(live_edge, edge_dst[relation], -1)]
    another operation x38 -> x0, local copies, waits for them, and re-layouts: 3.78 us -> none  [the longest x4 2.71 us: serve_every(): jnp.stack(pieces)]
    another operation x14 -> x0, loops' own time: 2.21 us -> none  [pick_columns(): picked = lax.map(one_block, index.reshape(count // block_size, block_size))]
  transfers between devices with their start and end apart: 2 -> 0, of which waited for: 2 -> 0; matrix products, arithmetic and copies ran while one was open for 6% -> 0% of each run, Pallas kernels for 0% -> 0%
where the time goes in v1:
time: 70.9 us; the launch traced here: 70.8 us
  Pallas kernels  69.3 us (98%)
  local copies, waits for them, and re-layouts  1.42 us (2%)
    pallas_call x1, Pallas kernels, per_device(): pl.pallas_call(functools.partial(kernel, n_mp), out_shape=jax.ShapeDtypeS...  69.3 us
    unnamed x1, local copies, waits for them, and re-layouts  1.42 us

profile of v1, /device:TPU:1, one launch (start us, length us, event | category | flops | bytes accessed | tf_op | source)
XLA Modules:
  0.0 70.8 jit_solution(1345790472726182426)
XLA Ops:
  0.0 69.3 %shard_map.73 = bf16[3,64,128]{2,1,0:T(8,128)(2,1)} custom-call(bf16[3,64,2048]{2,1,0:T(8,128)(2,1)} %feat.1, bf16[11,64,512]{2,1,0:T(8,128)(2,1)} %w.1, s32[3,1,2048]{2,1,0:T(1,128)} %bitcast.2, s32[3,2048]{1,0:T(4,128)} %row.1, s32[8,2048]{1,0:T(8,128)} %esrc.1, s32[8,2048]{1,0:T(8,128)} %edst.1, s32[1,8]{1,0:T(1,128)} %bitcast.3), custom_call_target="tpu_custom_call" | custom-call | tf_op jit(solution)/shard_map/pallas_call | solution.py:245
  69.4 1.4 %copy.9 = bf16[3,64,128]{2,1,0:T(8,128)(2,1)} copy(bf16[3,64,128]{2,1,0:T(8,128)(2,1)} %shard_map.73) | data formatting | bytes 98304

commit v2 on v1

v2 whole, which is shorter than its diff:
```python
import jax
import jax.numpy as jnp
from jax import lax
from jax.experimental import pallas as pl
from jax.experimental.pallas import tpu as pltpu
from jax.sharding import PartitionSpec as P

TYPES = 3
RELS = 8
SEEDS = 128
CAP = 128
RELATION_SOURCE = (0, 1, 0, 1, 2, 0, 2, 1)
STACKS = ((1, 2, 6, 8), (0, 4, 7, 9), (3, 5, 10))
NZ, NY = 8, 4
DP = NZ * NY
MESH = pl.DeviceIdType.MESH
F32, BF16, I32 = jnp.float32, jnp.bfloat16, jnp.int32
EB = 512


def iota(shape, dim):
    return lax.broadcasted_iota(I32, shape, dim)


def hot(ids, rows):
    return (iota((rows, ids.shape[1]), 0) == ids).astype(F32).astype(BF16)


def dot(a, b):
    return jnp.dot(a, b, preferred_element_type=F32)


def dot_nt(a, b):
    return lax.dot_general(a, b, (((1,), (1,)), ((), ())), preferred_element_type=F32)


def hops(o):
    return min(o[0], NZ - o[0]) + min(o[1], NY - o[1])


OFFSETS = [(dz, dy) for dz in range(NZ) for dy in range(NY)]
NEAREST = sorted(OFFSETS, key=lambda o: (hops(o), o[1], o[0]))
PLANES = (4, 3, 5, 2, 6, 1, 7, 0)
LAST = 2
LAST_RELS = tuple(r for r in range(RELS) if RELATION_SOURCE[r] == LAST)


def kernel(feat_h, w_h, own_h, row_h, esrc_h, edst_h, ecnt_h, out,
           feat, w, own, row, esrc, edst, ecnt,
           rq, req_out, req_in, send, recv, lk, pc, plo, lohot, counts, deg, msgs, wt,
           psend, pair, comb, final, ins, rs, rr, ss, sr, ds, dr, ps, pr):
    me, mm = lax.axis_index("dp"), lax.axis_index("mp")
    z, y = me // NY, me % NY
    x, core = mm // 2, mm % 2
    nx = final.shape[1]

    def fwd(o):
        return ((z + o[0]) % NZ) * NY + (y + o[1]) % NY

    def bwd(o):
        return ((z + NZ - o[0]) % NZ) * NY + (y + NY - o[1]) % NY

    def sem(o):
        return o[0] * NY + o[1]

    barrier = pltpu.get_barrier_semaphore()
    for o in NEAREST[:0:-1]:
        pl.semaphore_signal(barrier, 1, device_id={"dp": fwd(o)}, device_id_type=MESH)
    sibling = x * 2 + (1 - core)
    pl.semaphore_signal(barrier, 1, device_id={"mp": sibling}, device_id_type=MESH)

    def along_x(d):
        return ((x + d) % nx) * 2 + core

    for d in range(1, nx):
        pl.semaphore_signal(barrier, 1, device_id={"mp": along_x(d)}, device_id_type=MESH)

    loads = [
        pltpu.make_async_copy(src, dst, ins.at[i])
        for i, (src, dst) in enumerate((
            (own_h, own), (row_h, row), (feat_h, feat), (esrc_h, esrc), (edst_h, edst),
            (ecnt_h, ecnt), (w_h, w)))
    ]
    for load in loads:
        load.start()

    upper = (iota((256, 256), 0) <= iota((256, 256), 1)).astype(F32).astype(BF16)
    base = jnp.zeros((TYPES * DP, 1), F32)
    acc = [jnp.zeros((2 * DP, CAP), F32) for _ in range(TYPES)]
    loads[0].wait()
    loads[1].wait()
    for blk in range(8):
        lanes = slice(blk * 256, (blk + 1) * 256)
        owners = [own[t, :, lanes] for t in range(TYPES)]
        ohs = [(iota((DP, 256), 0) == owners[t]).astype(F32) for t in range(TYPES)]
        oh = jnp.concatenate(ohs, axis=0)
        incl = dot(oh.astype(BF16), upper) + base
        base = incl[:, 255:256]
        ranked = oh * (incl - 1.0)
        for t in range(TYPES):
            rank = jnp.sum(ranked[t * DP:(t + 1) * DP], axis=0, keepdims=True).astype(I32)
            ids = row[t:t + 1, lanes]
            left = jnp.concatenate(
                [ohs[t] * (ids >> 8).astype(F32), ohs[t] * (ids & 255).astype(F32)], axis=0
            ).astype(BF16)
            acc[t] = acc[t] + dot_nt(left, hot(rank, CAP))
            lk[t, blk:blk + 1, :] = (owners[t] >> 1).astype(F32)
            lk[t, 8 + blk:9 + blk, :] = ((owners[t] & 1) * CAP + rank).astype(F32)
    for t in range(TYPES):
        rq[t * DP:(t + 1) * DP, :] = (acc[t][:DP] * 256.0 + acc[t][DP:]).astype(I32)
    for o in range(DP):
        req_out[o, :, :] = rq[pl.ds(o, TYPES, stride=DP), :]

    pl.semaphore_wait(barrier, DP - 1 + nx)

    def req_copy(o):
        return pltpu.make_async_remote_copy(
            req_out.at[fwd(o)], req_in.at[me], rs.at[sem(o)], rr.at[sem(o)],
            device_id={"dp": fwd(o)}, device_id_type=MESH)

    for o in NEAREST[:0:-1]:
        req_copy(o).start()
    req_in[me] = req_out[me]

    def row_copy(t, o):
        return pltpu.make_async_remote_copy(
            send.at[t, bwd(o)], recv.at[t, me], ss.at[t, sem(o)], sr.at[t, sem(o)],
            device_id={"dp": bwd(o)}, device_id_type=MESH)

    asked = {(0, 0)}

    def serve(t, group):
        for o in group:
            if o not in asked:
                req_copy(o).wait_recv()
                asked.add(o)
        peers = [bwd(o) for o in group]
        ids = jnp.concatenate([req_in[p, t:t + 1, :] for p in peers], axis=1)
        low, high = ids & 255, ids >> 8
        table = jnp.concatenate([feat[t, :, c * 256:(c + 1) * 256] for c in range(8)], axis=0)
        res = dot(table, hot(low, 256))
        picked = res[0:64]
        for c in range(1, 8):
            picked = jnp.where(high == c, res[c * 64:(c + 1) * 64], picked)
        picked = picked.astype(BF16)
        for j, o in enumerate(group):
            piece = picked[:, j * CAP:(j + 1) * CAP]
            if o == (0, 0):
                recv[t, me] = piece
            else:
                send[t, peers[j]] = piece
        for o in group:
            if o != (0, 0):
                row_copy(t, o).start()

    groups = [NEAREST[4 * g:4 * g + 4] for g in range(8)]
    loads[2].wait()
    for t, gs in ((0, groups[:4]), (1, groups[:4]), (0, groups[4:]), (1, groups[4:])):
        for g in gs:
            serve(t, g)
    for dz in PLANES:
        serve(LAST, [(dz, dy) for dy in range(NY)])

    loads[3].wait()
    for r in range(RELS):
        t = RELATION_SOURCE[r]

        def look(k, _, r=r, t=t):
            lanes = pl.ds(pl.multiple_of(k * EB, EB), EB)
            src = esrc[r:r + 1, lanes]
            res = dot(lk[t].astype(BF16), hot(src & 255, 256))
            here = iota((8, EB), 0) == (src >> 8)
            pc[r:r + 1, lanes] = jnp.sum(jnp.where(here, res[:8], 0.0), axis=0, keepdims=True)
            plo[r:r + 1, lanes] = jnp.sum(jnp.where(here, res[8:], 0.0), axis=0, keepdims=True)
            return 0

        lax.fori_loop(0, 2048 // EB, look, 0)
    loads[4].wait()
    loads[5].wait()
    loads[6].wait()

    for i, r in enumerate(LAST_RELS):
        slot = iota((1, 2048), 1)
        target = jnp.where(slot < ecnt[0, r], edst[r:r + 1, :], -1)
        deg[i] = dot_nt(jnp.ones((16, 2048), BF16), hot(target, SEEDS))
        lohot[...] = hot(plo[r:r + 1, :].astype(I32), 256)

        def count(n, _, i=i, r=r):
            slot = iota((1, 2048), 1)
            pair_id = jnp.where(slot < ecnt[0, r],
                                pc[r:r + 1, :].astype(I32) * SEEDS + edst[r:r + 1, :] - n * 256, -1)
            res = dot_nt(lohot[...], hot(pair_id, 256)).astype(BF16)
            counts[2 * n, :, i * SEEDS:(i + 1) * SEEDS] = res[:, :SEEDS]
            counts[2 * n + 1, :, i * SEEDS:(i + 1) * SEEDS] = res[:, SEEDS:]
            return 0

        lax.fori_loop(0, 8, count, 0)
    for c in range(16):
        seed = jnp.where(lk[LAST, 0:1, 0:SEEDS] == float(c), lk[LAST, 8:9, 0:SEEDS], -1.0)
        counts[c, :, 256:384] = hot(seed.astype(I32), 256)

    for a in range(TYPES):
        mats = [w[m].astype(F32) for m in STACKS[a]]
        if len(mats) < 4:
            mats.append(jnp.zeros_like(mats[0]))
            msgs[a, 192:256, :] = jnp.zeros((64, SEEDS), BF16)
        wt[a] = jnp.concatenate(mats, axis=0).T.astype(BF16)

    def landed(t, c):
        return jnp.concatenate([recv[t, 2 * c], recv[t, 2 * c + 1]], axis=1)

    def pick(t, chunk, low):
        oh = hot(low.astype(I32), 256)
        picked = None
        for g in range(4):
            left = jnp.concatenate([landed(t, c) for c in range(4 * g, 4 * g + 4)], axis=0)
            res = dot(left, oh)
            for k in range(4):
                part = res[k * 64:(k + 1) * 64]
                picked = part if picked is None else jnp.where(chunk == float(4 * g + k), part, picked)
        return picked.astype(BF16)

    def put(m, value):
        for a in range(TYPES):
            if m in STACKS[a]:
                k = STACKS[a].index(m) * 64
                msgs[a, k:k + 64, :] = value.astype(BF16)

    for t in range(LAST):
        for o in NEAREST[1:]:
            row_copy(t, o).wait_recv()
        put(RELS + t, pick(t, lk[t, 0:1, 0:SEEDS], lk[t, 8:9, 0:SEEDS]))
        for r in range(RELS):
            if RELATION_SOURCE[r] != t:
                continue
            live = ecnt[0, r]

            def edges(k, total, r=r, t=t, live=live):
                lanes = pl.ds(pl.multiple_of(k * EB, EB), EB)
                rows = pick(t, pc[r:r + 1, lanes], plo[r:r + 1, lanes])
                rows = jnp.concatenate([rows, jnp.ones((16, EB), BF16)], axis=0)
                slot = iota((1, EB), 1) + k * EB
                target = jnp.where(slot < live, edst[r:r + 1, lanes], -1)
                return total + dot_nt(rows, hot(target, SEEDS))

            total = lax.fori_loop(0, 2048 // EB, edges, jnp.zeros((80, SEEDS), F32))
            put(r, total[:64] / jnp.maximum(total[64:65], 1.0))

    total = jnp.zeros((64, 384), F32)
    for dz in PLANES:
        for dy in range(NY):
            if (dz, dy) != (0, 0):
                row_copy(LAST, (dz, dy)).wait_recv()
        for h in range(2):
            c = ((z + dz) % NZ) * 2 + h
            total = total + dot(landed(LAST, c), counts[c])
    for i, r in enumerate(LAST_RELS):
        put(r, total[:, i * SEEDS:(i + 1) * SEEDS] / jnp.maximum(deg[i, 0:1, :], 1.0))
    put(RELS + LAST, total[:, 256:384])

    def pair_copy(a):
        return pltpu.make_async_remote_copy(
            psend.at[a, 1 - core], pair.at[a], ds.at[a], dr.at[a],
            device_id={"mp": sibling}, device_id_type=MESH)

    def part_copy(a, d):
        return pltpu.make_async_remote_copy(
            comb.at[a, (x + d) % nx], final.at[a, x], ps.at[a, d], pr.at[a, d],
            device_id={"mp": along_x(d)}, device_id_type=MESH)

    for a in range(TYPES):
        part = dot(wt[a], msgs[a]).astype(BF16)
        for p in range(2 * nx):
            psend[a, p % 2, p // 2] = part[p * 64:(p + 1) * 64]
        pair_copy(a).start()
    for a in range(TYPES):
        pair_copy(a).wait_recv()
        comb[a] = (psend[a, core].astype(F32) + pair[a].astype(F32)).astype(BF16)
        for d in range(1, nx):
            part_copy(a, d).start()
        final[a, x] = comb[a, x]
    for a in range(TYPES):
        for d in range(1, nx):
            part_copy(a, d).wait_recv()
        typed = final[a, 0].astype(F32)
        for p in range(1, nx):
            typed = typed + final[a, p].astype(F32)
        out[a] = jnp.maximum(typed, 0.0).astype(BF16)

    for o in NEAREST[1:]:
        req_copy(o).wait_send()
        for t in range(TYPES):
            row_copy(t, o).wait_send()
    for a in range(TYPES):
        pair_copy(a).wait_send()
        for d in range(1, nx):
            part_copy(a, d).wait_send()


def solution(mesh):
    n_mp = mesh.shape["mp"]

    def per_device(features, weights, sample_owner, sample_row, edge_src, edge_dst, edge_count):
        nx = n_mp // 2
        return pl.pallas_call(
            kernel,
            out_shape=jax.ShapeDtypeStruct((TYPES, 64, SEEDS), BF16),
            in_specs=[pl.BlockSpec(memory_space=pltpu.HBM)] * 7,
            out_specs=pl.BlockSpec(memory_space=pltpu.VMEM),
            scratch_shapes=[
                pltpu.VMEM((TYPES, 64, 2048), BF16),
                pltpu.VMEM((11, 64, 512), BF16),
                pltpu.VMEM((TYPES, 1, 2048), I32),
                pltpu.VMEM((TYPES, 2048), I32),
                pltpu.VMEM((RELS, 2048), I32),
                pltpu.VMEM((RELS, 2048), I32),
                pltpu.SMEM((1, RELS), I32),
                pltpu.VMEM((TYPES * DP, CAP), I32),
                pltpu.VMEM((DP, TYPES, CAP), I32),
                pltpu.VMEM((DP, TYPES, CAP), I32),
                pltpu.VMEM((TYPES, DP, 64, CAP), BF16),
                pltpu.VMEM((TYPES, DP, 64, CAP), BF16),
                pltpu.VMEM((TYPES, 16, 256), F32),
                pltpu.VMEM((RELS, 2048), F32),
                pltpu.VMEM((RELS, 2048), F32),
                pltpu.VMEM((256, 2048), BF16),
                pltpu.VMEM((16, 256, 384), BF16),
                pltpu.VMEM((len(LAST_RELS), 16, SEEDS), F32),
                pltpu.VMEM((TYPES, 256, SEEDS), BF16),
                pltpu.VMEM((TYPES, 512, 256), BF16),
                pltpu.VMEM((TYPES, 2, nx, 64, SEEDS), BF16),
                pltpu.VMEM((TYPES, nx, 64, SEEDS), BF16),
                pltpu.VMEM((TYPES, nx, 64, SEEDS), BF16),
                pltpu.VMEM((TYPES, nx, 64, SEEDS), BF16),
                pltpu.SemaphoreType.DMA((7,)),
                pltpu.SemaphoreType.DMA((DP,)),
                pltpu.SemaphoreType.DMA((DP,)),
                pltpu.SemaphoreType.DMA((TYPES, DP)),
                pltpu.SemaphoreType.DMA((TYPES, DP)),
                pltpu.SemaphoreType.DMA((TYPES,)),
                pltpu.SemaphoreType.DMA((TYPES,)),
                pltpu.SemaphoreType.DMA((TYPES, nx)),
                pltpu.SemaphoreType.DMA((TYPES, nx)),
            ],
            compiler_params=pltpu.CompilerParams(
                collective_id=0, has_side_effects=True, vmem_limit_bytes=60000000),
        )(features, weights, jnp.transpose(sample_owner, (0, 2, 1)), sample_row,
          edge_src, edge_dst, jnp.transpose(edge_count, (1, 0)))

    return jax.shard_map(
        per_device,
        mesh=mesh,
        in_specs=(
            P(None, "mp", "dp"),
            P(None, "mp", None),
            P(None, "dp", None),
            P(None, "dp"),
            P(None, "dp"),
            P(None, "dp"),
            P(None, "dp"),
        ),
        out_specs=P(None, "mp", "dp"),
        check_vma=False,
    )
```

time: 70.9 us -> 65.8 us (0.928)
  Pallas kernels: 69.3 us -> 64.3 us
    pallas_call x1, Pallas kernels: 69.3 us -> 64.3 us  [per_device(): pl.pallas_call(kernel, out_shape=jax.ShapeDtypeStruct((TYPES, 64, SEEDS),...]
where the time goes in v2:
time: 65.8 us; the launch traced here: 65.7 us
  Pallas kernels  64.3 us (98%)
  local copies, waits for them, and re-layouts  1.42 us (2%)
    pallas_call x1, Pallas kernels, per_device(): pl.pallas_call(kernel, out_shape=jax.ShapeDtypeStruct((TYPES, 64, SEEDS),...  64.3 us
    unnamed x1, local copies, waits for them, and re-layouts  1.42 us

profile of v2, /device:TPU:1, one launch (start us, length us, event | category | flops | bytes accessed | tf_op | source)
XLA Modules:
  0.0 65.7 jit_solution(6387692459061189127)
XLA Ops:
  0.0 64.3 %shard_map.73 = bf16[3,64,128]{2,1,0:T(8,128)(2,1)} custom-call(bf16[3,64,2048]{2,1,0:T(8,128)(2,1)} %feat_h.1, bf16[11,64,512]{2,1,0:T(8,128)(2,1)} %w_h.1, s32[3,1,2048]{2,1,0:T(1,128)} %bitcast.2, s32[3,2048]{1,0:T(4,128)} %row_h.1, s32[8,2048]{1,0:T(8,128)} %esrc_h.1, s32[8,2048]{1,0:T(8,128)} %edst_h.1, s32[1,8]{1,0:T(1,128)} %bitcast.3), custom_call_target="tpu_custom_call" | custom-call | tf_op jit(solution)/shard_map/pallas_call | solution.py:305
  64.3 1.4 %copy.9 = bf16[3,64,128]{2,1,0:T(8,128)(2,1)} copy(bf16[3,64,128]{2,1,0:T(8,128)(2,1)} %shard_map.73) | data formatting | bytes 98304

commit v3 on v2

--- a/solution.py
+++ b/solution.py
@@ -42,17 +42,20 @@
 NEAREST = sorted(OFFSETS, key=lambda o: (hops(o), o[1], o[0]))
 PLANES = (4, 3, 5, 2, 6, 1, 7, 0)
 LAST = 2
+PARTS = 2
+PART = 64 // PARTS
+PIECES = 8 + 3 * PARTS
+FARTHEST = (4, 3, 5, 2, 6, 1, 7)
 LAST_RELS = tuple(r for r in range(RELS) if RELATION_SOURCE[r] == LAST)
 
 
 def kernel(feat_h, w_h, own_h, row_h, esrc_h, edst_h, ecnt_h, out,
            feat, w, own, row, esrc, edst, ecnt,
            rq, req_out, req_in, send, recv, lk, pc, plo, lohot, counts, deg, msgs, wt,
-           psend, pair, comb, final, ins, rs, rr, ss, sr, ds, dr, ps, pr):
+           wfull, mfull, ins, rs, rr, ss, sr, ls, lr, ws, wr, ms, mr):
     me, mm = lax.axis_index("dp"), lax.axis_index("mp")
     z, y = me // NY, me % NY
-    x, core = mm // 2, mm % 2
-    nx = final.shape[1]
+    n_mp = mfull.shape[1]
 
     def fwd(o):
         return ((z + o[0]) % NZ) * NY + (y + o[1]) % NY
@@ -66,14 +69,8 @@
     barrier = pltpu.get_barrier_semaphore()
     for o in NEAREST[:0:-1]:
         pl.semaphore_signal(barrier, 1, device_id={"dp": fwd(o)}, device_id_type=MESH)
-    sibling = x * 2 + (1 - core)
-    pl.semaphore_signal(barrier, 1, device_id={"mp": sibling}, device_id_type=MESH)
-
-    def along_x(d):
-        return ((x + d) % nx) * 2 + core
-
-    for d in range(1, nx):
-        pl.semaphore_signal(barrier, 1, device_id={"mp": along_x(d)}, device_id_type=MESH)
+    for d in range(1, n_mp):
+        pl.semaphore_signal(barrier, 1, device_id={"mp": (mm + d) % n_mp}, device_id_type=MESH)
 
     loads = [
         pltpu.make_async_copy(src, dst, ins.at[i])
@@ -111,7 +108,7 @@
     for o in range(DP):
         req_out[o, :, :] = rq[pl.ds(o, TYPES, stride=DP), :]
 
-    pl.semaphore_wait(barrier, DP - 1 + nx)
+    pl.semaphore_wait(barrier, DP - 1 + n_mp - 1)
 
     def req_copy(o):
         return pltpu.make_async_remote_copy(
@@ -125,6 +122,13 @@
     def row_copy(t, o):
         return pltpu.make_async_remote_copy(
             send.at[t, bwd(o)], recv.at[t, me], ss.at[t, sem(o)], sr.at[t, sem(o)],
+            device_id={"dp": bwd(o)}, device_id_type=MESH)
+
+    def last_copy(h, o):
+        rows = pl.ds(h * PART, PART)
+        return pltpu.make_async_remote_copy(
+            send.at[LAST, bwd(o), rows, :], recv.at[LAST, me, rows, :],
+            ls.at[h, sem(o)], lr.at[h, sem(o)],
             device_id={"dp": bwd(o)}, device_id_type=MESH)
 
     asked = {(0, 0)}
@@ -151,7 +155,7 @@
                 send[t, peers[j]] = piece
         for o in group:
             if o != (0, 0):
-                row_copy(t, o).start()
+                (last_copy(0, o) if t == LAST else row_copy(t, o)).start()
 
     groups = [NEAREST[4 * g:4 * g + 4] for g in range(8)]
     loads[2].wait()
@@ -160,6 +164,29 @@
             serve(t, g)
     for dz in PLANES:
         serve(LAST, [(dz, dy) for dy in range(NY)])
+    for h in range(1, PARTS):
+        for dz in PLANES:
+            for dy in range(NY):
+                if (dz, dy) != (0, 0):
+                    last_copy(h, (dz, dy)).start()
+
+    def w_copy(a, d):
+        p = (mm + d) % n_mp
+        return pltpu.make_async_remote_copy(
+            wt.at[a, pl.ds(pl.multiple_of(p * 64, 64), 64), :], wfull.at[a, mm],
+            ws.at[a, d], wr.at[a, d], device_id={"mp": p}, device_id_type=MESH)
+
+    loads[6].wait()
+    for a in range(TYPES):
+        mats = [w[m].astype(F32) for m in STACKS[a]]
+        if len(mats) < 4:
+            mats.append(jnp.zeros_like(mats[0]))
+            for p in range(n_mp):
+                mfull[a, p, 192:256, :] = jnp.zeros((64, SEEDS), BF16)
+        wt[a] = jnp.concatenate(mats, axis=0).T.astype(BF16)
+        for d in FARTHEST:
+            w_copy(a, d).start()
+        wfull[a, mm] = wt[a, pl.ds(pl.multiple_of(mm * 64, 64), 64), :]
 
     loads[3].wait()
     for r in range(RELS):
@@ -177,7 +204,6 @@
         lax.fori_loop(0, 2048 // EB, look, 0)
     loads[4].wait()
     loads[5].wait()
-    loads[6].wait()
 
     for i, r in enumerate(LAST_RELS):
         slot = iota((1, 2048), 1)
@@ -198,13 +224,6 @@
     for c in range(16):
         seed = jnp.where(lk[LAST, 0:1, 0:SEEDS] == float(c), lk[LAST, 8:9, 0:SEEDS], -1.0)
         counts[c, :, 256:384] = hot(seed.astype(I32), 256)
-
-    for a in range(TYPES):
-        mats = [w[m].astype(F32) for m in STACKS[a]]
-        if len(mats) < 4:
-            mats.append(jnp.zeros_like(mats[0]))
-            msgs[a, 192:256, :] = jnp.zeros((64, SEEDS), BF16)
-        wt[a] = jnp.concatenate(mats, axis=0).T.astype(BF16)
 
     def landed(t, c):
         return jnp.concatenate([recv[t, 2 * c], recv[t, 2 * c + 1]], axis=1)
@@ -220,11 +239,26 @@
                 picked = part if picked is None else jnp.where(chunk == float(4 * g + k), part, picked)
         return picked.astype(BF16)
 
-    def put(m, value):
+    pieces = []
+
+    def m_copy(i, d):
+        a, k, n = pieces[i]
+        p = (mm + d) % n_mp
+        return pltpu.make_async_remote_copy(
+            msgs.at[a, pl.ds(k, n), :], mfull.at[a, mm, pl.ds(k, n), :],
+            ms.at[i, d], mr.at[i, d], device_id={"mp": p}, device_id_type=MESH)
+
+    def put(m, value, part=0):
         for a in range(TYPES):
             if m in STACKS[a]:
-                k = STACKS[a].index(m) * 64
-                msgs[a, k:k + 64, :] = value.astype(BF16)
+                n = value.shape[0]
+                k = STACKS[a].index(m) * 64 + part * n
+                value = value.astype(BF16)
+                msgs[a, k:k + n, :] = value
+                mfull[a, mm, k:k + n, :] = value
+                pieces.append((a, k, n))
+                for d in FARTHEST:
+                    m_copy(len(pieces) - 1, d).start()
 
     for t in range(LAST):
         for o in NEAREST[1:]:
@@ -246,65 +280,53 @@
             total = lax.fori_loop(0, 2048 // EB, edges, jnp.zeros((80, SEEDS), F32))
             put(r, total[:64] / jnp.maximum(total[64:65], 1.0))
 
-    total = jnp.zeros((64, 384), F32)
-    for dz in PLANES:
-        for dy in range(NY):
-            if (dz, dy) != (0, 0):
-                row_copy(LAST, (dz, dy)).wait_recv()
-        for h in range(2):
-            c = ((z + dz) % NZ) * 2 + h
-            total = total + dot(landed(LAST, c), counts[c])
-    for i, r in enumerate(LAST_RELS):
-        put(r, total[:, i * SEEDS:(i + 1) * SEEDS] / jnp.maximum(deg[i, 0:1, :], 1.0))
-    put(RELS + LAST, total[:, 256:384])
-
-    def pair_copy(a):
-        return pltpu.make_async_remote_copy(
-            psend.at[a, 1 - core], pair.at[a], ds.at[a], dr.at[a],
-            device_id={"mp": sibling}, device_id_type=MESH)
-
-    def part_copy(a, d):
-        return pltpu.make_async_remote_copy(
-            comb.at[a, (x + d) % nx], final.at[a, x], ps.at[a, d], pr.at[a, d],
-            device_id={"mp": along_x(d)}, device_id_type=MESH)
-
+    for h in range(PARTS):
+        total = jnp.zeros((PART, 384), F32)
+        for dz in PLANES:
+            for dy in range(NY):
+                if (dz, dy) != (0, 0):
+                    last_copy(h, (dz, dy)).wait_recv()
+            for half in range(2):
+                c = ((z + dz) % NZ) * 2 + half
+                rows = slice(h * PART, (h + 1) * PART)
+                left = jnp.concatenate(
+                    [recv[LAST, 2 * c, rows, :], recv[LAST, 2 * c + 1, rows, :]], axis=1)
+                total = total + dot(left, counts[c])
+        for i, r in enumerate(LAST_RELS):
+            put(r, total[:, i * SEEDS:(i + 1) * SEEDS] / jnp.maximum(deg[i, 0:1, :], 1.0), h)
+        put(RELS + LAST, total[:, 256:384], h)
+
+    for d in FARTHEST[::-1]:
+        for a in range(TYPES):
+            w_copy(a, d).wait_recv()
+        for i in range(len(pieces)):
+            m_copy(i, d).wait_recv()
     for a in range(TYPES):
-        part = dot(wt[a], msgs[a]).astype(BF16)
-        for p in range(2 * nx):
-            psend[a, p % 2, p // 2] = part[p * 64:(p + 1) * 64]
-        pair_copy(a).start()
-    for a in range(TYPES):
-        pair_copy(a).wait_recv()
-        comb[a] = (psend[a, core].astype(F32) + pair[a].astype(F32)).astype(BF16)
-        for d in range(1, nx):
-            part_copy(a, d).start()
-        final[a, x] = comb[a, x]
-    for a in range(TYPES):
-        for d in range(1, nx):
-            part_copy(a, d).wait_recv()
-        typed = final[a, 0].astype(F32)
-        for p in range(1, nx):
-            typed = typed + final[a, p].astype(F32)
+        typed = dot(wfull[a, 0], mfull[a, 0])
+        for p in range(1, n_mp):
+            typed = typed + dot(wfull[a, p], mfull[a, p])
         out[a] = jnp.maximum(typed, 0.0).astype(BF16)
 
     for o in NEAREST[1:]:
         req_copy(o).wait_send()
-        for t in range(TYPES):
+        for t in range(LAST):
             row_copy(t, o).wait_send()
-    for a in range(TYPES):
-        pair_copy(a).wait_send()
-        for d in range(1, nx):
-            part_copy(a, d).wait_send()
+        for h in range(PARTS):
+            last_copy(h, o).wait_send()
+    for d in FARTHEST:
+        for a in range(TYPES):
+            w_copy(a, d).wait_send()
+        for i in range(len(pieces)):
+            m_copy(i, d).wait_send()
 
 
 def solution(mesh):
     n_mp = mesh.shape["mp"]
 
     def per_device(features, weights, sample_owner, sample_row, edge_src, edge_dst, edge_count):
-        nx = n_mp // 2
         return pl.pallas_call(
             kernel,
-            out_shape=jax.ShapeDtypeStruct((TYPES, 64, SEEDS), BF16),
+            out_shape=pltpu.VMEM((TYPES, 64, SEEDS), BF16),
             in_specs=[pl.BlockSpec(memory_space=pltpu.HBM)] * 7,
             out_specs=pl.BlockSpec(memory_space=pltpu.VMEM),
             scratch_shapes=[
@@ -328,19 +350,19 @@
                 pltpu.VMEM((len(LAST_RELS), 16, SEEDS), F32),
                 pltpu.VMEM((TYPES, 256, SEEDS), BF16),
                 pltpu.VMEM((TYPES, 512, 256), BF16),
-                pltpu.VMEM((TYPES, 2, nx, 64, SEEDS), BF16),
-                pltpu.VMEM((TYPES, nx, 64, SEEDS), BF16),
-                pltpu.VMEM((TYPES, nx, 64, SEEDS), BF16),
-                pltpu.VMEM((TYPES, nx, 64, SEEDS), BF16),
+                pltpu.VMEM((TYPES, n_mp, 64, 256), BF16),
+                pltpu.VMEM((TYPES, n_mp, 256, SEEDS), BF16),
                 pltpu.SemaphoreType.DMA((7,)),
                 pltpu.SemaphoreType.DMA((DP,)),
                 pltpu.SemaphoreType.DMA((DP,)),
-                pltpu.SemaphoreType.DMA((TYPES, DP)),
-                pltpu.SemaphoreType.DMA((TYPES, DP)),
-                pltpu.SemaphoreType.DMA((TYPES,)),
-                pltpu.SemaphoreType.DMA((TYPES,)),
-                pltpu.SemaphoreType.DMA((TYPES, nx)),
-                pltpu.SemaphoreType.DMA((TYPES, nx)),
+                pltpu.SemaphoreType.DMA((LAST, DP)),
+                pltpu.SemaphoreType.DMA((LAST, DP)),
+                pltpu.SemaphoreType.DMA((PARTS, DP)),
+                pltpu.SemaphoreType.DMA((PARTS, DP)),
+                pltpu.SemaphoreType.DMA((TYPES, n_mp)),
+                pltpu.SemaphoreType.DMA((TYPES, n_mp)),
+                pltpu.SemaphoreType.DMA((PIECES, n_mp)),
+                pltpu.SemaphoreType.DMA((PIECES, n_mp)),
             ],
             compiler_params=pltpu.CompilerParams(
                 collective_id=0, has_side_effects=True, vmem_limit_bytes=60000000),

time: 65.8 us -> 68 us (1.033)
  Pallas kernels: 64.3 us -> 67.2 us
  local copies, waits for them, and re-layouts: 1.42 us -> 0.62 us
    pallas_call x1, Pallas kernels: 64.3 us -> 67.2 us  [per_device(): pl.pallas_call(kernel, out_shape=pltpu.VMEM((TYPES, 64, SEEDS), BF16), in...]
    unnamed x1, local copies, waits for them, and re-layouts: 1.42 us -> 0.62 us
where the time goes in v3:
time: 68 us; the launch traced here: 67.9 us
  Pallas kernels  67.2 us (99%)
    pallas_call x1, Pallas kernels, per_device(): pl.pallas_call(kernel, out_shape=pltpu.VMEM((TYPES, 64, SEEDS), BF16), in...  67.2 us

profile of v3, /device:TPU:1, one launch (start us, length us, event | category | flops | bytes accessed | tf_op | source)
XLA Modules:
  0.0 67.9 jit_solution(8265881796803541889)
XLA Ops:
  0.0 67.2 %shard_map.73 = bf16[3,64,128]{2,1,0:T(8,128)(2,1)S(1)} custom-call(bf16[3,64,2048]{2,1,0:T(8,128)(2,1)} %feat_h.1, bf16[11,64,512]{2,1,0:T(8,128)(2,1)} %w_h.1, s32[3,1,2048]{2,1,0:T(1,128)} %bitcast.2, s32[3,2048]{1,0:T(4,128)} %row_h.1, s32[8,2048]{1,0:T(8,128)} %esrc_h.1, s32[8,2048]{1,0:T(8,128)} %edst_h.1, s32[1,8]{1,0:T(1,128)} %bitcast.3), custom_call_target="tpu_custom_call" | custom-call | tf_op jit(solution)/shard_map/pallas_call | solution.py:327
  67.2 0.6 copy.9

commit v4 on v2

--- a/solution.py
+++ b/solution.py
@@ -48,11 +48,10 @@
 def kernel(feat_h, w_h, own_h, row_h, esrc_h, edst_h, ecnt_h, out,
            feat, w, own, row, esrc, edst, ecnt,
            rq, req_out, req_in, send, recv, lk, pc, plo, lohot, counts, deg, msgs, wt,
-           psend, pair, comb, final, ins, rs, rr, ss, sr, ds, dr, ps, pr):
+           gath, psend, precv, ins, rs, rr, ss, sr, lr, ps, pr):
     me, mm = lax.axis_index("dp"), lax.axis_index("mp")
     z, y = me // NY, me % NY
-    x, core = mm // 2, mm % 2
-    nx = final.shape[1]
+    n_mp = precv.shape[1]
 
     def fwd(o):
         return ((z + o[0]) % NZ) * NY + (y + o[1]) % NY
@@ -60,20 +59,18 @@
     def bwd(o):
         return ((z + NZ - o[0]) % NZ) * NY + (y + NY - o[1]) % NY
 
-    def sem(o):
-        return o[0] * NY + o[1]
+    groups = [NEAREST[4 * g:4 * g + 4] for g in range(8)]
+    batch = {o: g for g in range(8) for o in groups[g]}
+
+    def many(src, dst, send_sem, recv_sem):
+        return pltpu.make_async_remote_copy(
+            src, dst, send_sem, recv_sem, device_id={"dp": fwd((0, 1))}, device_id_type=MESH)
 
     barrier = pltpu.get_barrier_semaphore()
     for o in NEAREST[:0:-1]:
         pl.semaphore_signal(barrier, 1, device_id={"dp": fwd(o)}, device_id_type=MESH)
-    sibling = x * 2 + (1 - core)
-    pl.semaphore_signal(barrier, 1, device_id={"mp": sibling}, device_id_type=MESH)
-
-    def along_x(d):
-        return ((x + d) % nx) * 2 + core
-
-    for d in range(1, nx):
-        pl.semaphore_signal(barrier, 1, device_id={"mp": along_x(d)}, device_id_type=MESH)
+    for d in range(1, n_mp):
+        pl.semaphore_signal(barrier, 1, device_id={"mp": (mm + d) % n_mp}, device_id_type=MESH)
 
     loads = [
         pltpu.make_async_copy(src, dst, ins.at[i])
@@ -111,11 +108,11 @@
     for o in range(DP):
         req_out[o, :, :] = rq[pl.ds(o, TYPES, stride=DP), :]
 
-    pl.semaphore_wait(barrier, DP - 1 + nx)
+    pl.semaphore_wait(barrier, DP - 1 + n_mp - 1)
 
     def req_copy(o):
         return pltpu.make_async_remote_copy(
-            req_out.at[fwd(o)], req_in.at[me], rs.at[sem(o)], rr.at[sem(o)],
+            req_out.at[fwd(o)], req_in.at[me], rs.at[0], rr.at[batch[o]],
             device_id={"dp": fwd(o)}, device_id_type=MESH)
 
     for o in NEAREST[:0:-1]:
@@ -124,16 +121,17 @@
 
     def row_copy(t, o):
         return pltpu.make_async_remote_copy(
-            send.at[t, bwd(o)], recv.at[t, me], ss.at[t, sem(o)], sr.at[t, sem(o)],
+            send.at[t, bwd(o)], recv.at[t, me], ss.at[t],
+            lr.at[o[0]] if t == LAST else sr.at[t],
             device_id={"dp": bwd(o)}, device_id_type=MESH)
 
-    asked = {(0, 0)}
+    asked = set()
 
     def serve(t, group):
-        for o in group:
-            if o not in asked:
-                req_copy(o).wait_recv()
-                asked.add(o)
+        for g in sorted({batch[o] for o in group} - asked):
+            n = 3 if g == 0 else 4
+            many(req_out.at[0:n], req_in.at[0:n], rs.at[0], rr.at[g]).wait_recv()
+            asked.add(g)
         peers = [bwd(o) for o in group]
         ids = jnp.concatenate([req_in[p, t:t + 1, :] for p in peers], axis=1)
         low, high = ids & 255, ids >> 8
@@ -153,7 +151,6 @@
             if o != (0, 0):
                 row_copy(t, o).start()
 
-    groups = [NEAREST[4 * g:4 * g + 4] for g in range(8)]
     loads[2].wait()
     for t, gs in ((0, groups[:4]), (1, groups[:4]), (0, groups[4:]), (1, groups[4:])):
         for g in gs:
@@ -162,8 +159,8 @@
         serve(LAST, [(dz, dy) for dy in range(NY)])
 
     loads[3].wait()
-    for r in range(RELS):
-        t = RELATION_SOURCE[r]
+    for r in LAST_RELS:
+        t = LAST
 
         def look(k, _, r=r, t=t):
             lanes = pl.ds(pl.multiple_of(k * EB, EB), EB)
@@ -209,15 +206,13 @@
     def landed(t, c):
         return jnp.concatenate([recv[t, 2 * c], recv[t, 2 * c + 1]], axis=1)
 
-    def pick(t, chunk, low):
-        oh = hot(low.astype(I32), 256)
+    def select(oh, chunk, parts):
         picked = None
-        for g in range(4):
-            left = jnp.concatenate([landed(t, c) for c in range(4 * g, 4 * g + 4)], axis=0)
-            res = dot(left, oh)
+        for g in range(0, len(parts), 4):
+            res = dot(jnp.concatenate([part() for part in parts[g:g + 4]], axis=0), oh)
             for k in range(4):
                 part = res[k * 64:(k + 1) * 64]
-                picked = part if picked is None else jnp.where(chunk == float(4 * g + k), part, picked)
+                picked = part if picked is None else jnp.where(chunk == g + k, part, picked)
         return picked.astype(BF16)
 
     def put(m, value):
@@ -226,18 +221,33 @@
                 k = STACKS[a].index(m) * 64
                 msgs[a, k:k + 64, :] = value.astype(BF16)
 
+    def all_rows(t, sems):
+        return many(send.at[t, 0:DP - 1], recv.at[t, 0:DP - 1], ss.at[t], sems)
+
+    many(req_out.at[0:DP - 1], req_in.at[0:DP - 1], rs.at[0], rr.at[0]).wait_send()
     for t in range(LAST):
-        for o in NEAREST[1:]:
-            row_copy(t, o).wait_recv()
-        put(RELS + t, pick(t, lk[t, 0:1, 0:SEEDS], lk[t, 8:9, 0:SEEDS]))
+        all_rows(t, sr.at[t]).wait_recv()
+
+        def gather(k, _, t=t):
+            chunk, low = (
+                jnp.concatenate([lk[t, pl.ds(b + 2 * k, 1), :], lk[t, pl.ds(b + 2 * k + 1, 1), :]],
+                                axis=1).astype(I32) for b in (0, 8))
+            gath[:, pl.ds(pl.multiple_of(k * EB, EB), EB)] = select(
+                hot(low, 256), chunk, [lambda c=c: landed(t, c) for c in range(16)])
+            return 0
+
+        lax.fori_loop(0, 2048 // EB, gather, 0)
+        put(RELS + t, gath[:, 0:SEEDS])
         for r in range(RELS):
             if RELATION_SOURCE[r] != t:
                 continue
             live = ecnt[0, r]
 
-            def edges(k, total, r=r, t=t, live=live):
+            def edges(k, total, r=r, live=live):
                 lanes = pl.ds(pl.multiple_of(k * EB, EB), EB)
-                rows = pick(t, pc[r:r + 1, lanes], plo[r:r + 1, lanes])
+                src = esrc[r:r + 1, lanes]
+                rows = select(hot(src & 255, 256), src >> 8,
+                              [lambda c=c: gath[:, c * 256:(c + 1) * 256] for c in range(8)])
                 rows = jnp.concatenate([rows, jnp.ones((16, EB), BF16)], axis=0)
                 slot = iota((1, EB), 1) + k * EB
                 target = jnp.where(slot < live, edst[r:r + 1, lanes], -1)
@@ -245,12 +255,12 @@
 
             total = lax.fori_loop(0, 2048 // EB, edges, jnp.zeros((80, SEEDS), F32))
             put(r, total[:64] / jnp.maximum(total[64:65], 1.0))
+        all_rows(t, sr.at[t]).wait_send()
 
     total = jnp.zeros((64, 384), F32)
     for dz in PLANES:
-        for dy in range(NY):
-            if (dz, dy) != (0, 0):
-                row_copy(LAST, (dz, dy)).wait_recv()
+        n = NY - 1 if dz == 0 else NY
+        many(send.at[LAST, 0:n], recv.at[LAST, 0:n], ss.at[LAST], lr.at[dz]).wait_recv()
         for h in range(2):
             c = ((z + dz) % NZ) * 2 + h
             total = total + dot(landed(LAST, c), counts[c])
@@ -258,53 +268,36 @@
         put(r, total[:, i * SEEDS:(i + 1) * SEEDS] / jnp.maximum(deg[i, 0:1, :], 1.0))
     put(RELS + LAST, total[:, 256:384])
 
-    def pair_copy(a):
+    def part_copy(a, d):
+        p = (mm + d) % n_mp
         return pltpu.make_async_remote_copy(
-            psend.at[a, 1 - core], pair.at[a], ds.at[a], dr.at[a],
-            device_id={"mp": sibling}, device_id_type=MESH)
-
-    def part_copy(a, d):
-        return pltpu.make_async_remote_copy(
-            comb.at[a, (x + d) % nx], final.at[a, x], ps.at[a, d], pr.at[a, d],
-            device_id={"mp": along_x(d)}, device_id_type=MESH)
+            psend.at[a, p], precv.at[a, mm], ps.at[0], pr.at[a],
+            device_id={"mp": p}, device_id_type=MESH)
 
     for a in range(TYPES):
         part = dot(wt[a], msgs[a]).astype(BF16)
-        for p in range(2 * nx):
-            psend[a, p % 2, p // 2] = part[p * 64:(p + 1) * 64]
-        pair_copy(a).start()
+        for p in range(n_mp):
+            psend[a, p] = part[p * 64:(p + 1) * 64]
+        for d in (4, 3, 5, 2, 6, 1, 7):
+            part_copy(a, d).start()
+        precv[a, mm] = psend[a, mm]
+    all_rows(LAST, sr.at[0]).wait_send()
     for a in range(TYPES):
-        pair_copy(a).wait_recv()
-        comb[a] = (psend[a, core].astype(F32) + pair[a].astype(F32)).astype(BF16)
-        for d in range(1, nx):
-            part_copy(a, d).start()
-        final[a, x] = comb[a, x]
-    for a in range(TYPES):
-        for d in range(1, nx):
-            part_copy(a, d).wait_recv()
-        typed = final[a, 0].astype(F32)
-        for p in range(1, nx):
-            typed = typed + final[a, p].astype(F32)
+        many(psend.at[a, 0:n_mp - 1], precv.at[a, 0:n_mp - 1], ps.at[0], pr.at[a]).wait_recv()
+        typed = precv[a, 0].astype(F32)
+        for p in range(1, n_mp):
+            typed = typed + precv[a, p].astype(F32)
         out[a] = jnp.maximum(typed, 0.0).astype(BF16)
-
-    for o in NEAREST[1:]:
-        req_copy(o).wait_send()
-        for t in range(TYPES):
-            row_copy(t, o).wait_send()
-    for a in range(TYPES):
-        pair_copy(a).wait_send()
-        for d in range(1, nx):
-            part_copy(a, d).wait_send()
+    many(psend.at[:, 0:n_mp - 1], precv.at[:, 0:n_mp - 1], ps.at[0], pr.at[0]).wait_send()
 
 
 def solution(mesh):
     n_mp = mesh.shape["mp"]
 
     def per_device(features, weights, sample_owner, sample_row, edge_src, edge_dst, edge_count):
-        nx = n_mp // 2
         return pl.pallas_call(
             kernel,
-            out_shape=jax.ShapeDtypeStruct((TYPES, 64, SEEDS), BF16),
+            out_shape=pltpu.VMEM((TYPES, 64, SEEDS), BF16),
             in_specs=[pl.BlockSpec(memory_space=pltpu.HBM)] * 7,
             out_specs=pl.BlockSpec(memory_space=pltpu.VMEM),
             scratch_shapes=[
@@ -328,19 +321,17 @@
                 pltpu.VMEM((len(LAST_RELS), 16, SEEDS), F32),
                 pltpu.VMEM((TYPES, 256, SEEDS), BF16),
                 pltpu.VMEM((TYPES, 512, 256), BF16),
-                pltpu.VMEM((TYPES, 2, nx, 64, SEEDS), BF16),
-                pltpu.VMEM((TYPES, nx, 64, SEEDS), BF16),
-                pltpu.VMEM((TYPES, nx, 64, SEEDS), BF16),
-                pltpu.VMEM((TYPES, nx, 64, SEEDS), BF16),
+                pltpu.VMEM((64, 2048), BF16),
+                pltpu.VMEM((TYPES, n_mp, 64, SEEDS), BF16),
+                pltpu.VMEM((TYPES, n_mp, 64, SEEDS), BF16),
                 pltpu.SemaphoreType.DMA((7,)),
-                pltpu.SemaphoreType.DMA((DP,)),
-                pltpu.SemaphoreType.DMA((DP,)),
-                pltpu.SemaphoreType.DMA((TYPES, DP)),
-                pltpu.SemaphoreType.DMA((TYPES, DP)),
+                pltpu.SemaphoreType.DMA((1,)),
+                pltpu.SemaphoreType.DMA((8,)),
                 pltpu.SemaphoreType.DMA((TYPES,)),
+                pltpu.SemaphoreType.DMA((LAST,)),
+                pltpu.SemaphoreType.DMA((NZ,)),
+                pltpu.SemaphoreType.DMA((1,)),
                 pltpu.SemaphoreType.DMA((TYPES,)),
-                pltpu.SemaphoreType.DMA((TYPES, nx)),
-                pltpu.SemaphoreType.DMA((TYPES, nx)),
             ],
             compiler_params=pltpu.CompilerParams(
                 collective_id=0, has_side_effects=True, vmem_limit_bytes=60000000),

time: 65.8 us -> 60.6 us (0.921)
  Pallas kernels: 64.3 us -> 59.8 us
  local copies, waits for them, and re-layouts: 1.42 us -> 0.62 us
    pallas_call x1, Pallas kernels: 64.3 us -> 59.8 us  [per_device(): pl.pallas_call(kernel, out_shape=pltpu.VMEM((TYPES, 64, SEEDS), BF16), in...]
    unnamed x1, local copies, waits for them, and re-layouts: 1.42 us -> 0.62 us
where the time goes in v4:
time: 60.6 us; the launch traced here: 60.5 us
  Pallas kernels  59.8 us (99%)
  local copies, waits for them, and re-layouts  0.62 us (1%)
    pallas_call x1, Pallas kernels, per_device(): pl.pallas_call(kernel, out_shape=pltpu.VMEM((TYPES, 64, SEEDS), BF16), in...  59.8 us

profile of v4, /device:TPU:1, one launch (start us, length us, event | category | flops | bytes accessed | tf_op | source)
XLA Modules:
  0.0 60.5 jit_solution(9341235756642368042)
XLA Ops:
  0.0 59.8 %shard_map.73 = bf16[3,64,128]{2,1,0:T(8,128)(2,1)S(1)} custom-call(bf16[3,64,2048]{2,1,0:T(8,128)(2,1)} %feat_h.1, bf16[11,64,512]{2,1,0:T(8,128)(2,1)} %w_h.1, s32[3,1,2048]{2,1,0:T(1,128)} %bitcast.2, s32[3,2048]{1,0:T(4,128)} %row_h.1, s32[8,2048]{1,0:T(8,128)} %esrc_h.1, s32[8,2048]{1,0:T(8,128)} %edst_h.1, s32[1,8]{1,0:T(1,128)} %bitcast.3), custom_call_target="tpu_custom_call" | custom-call | tf_op jit(solution)/shard_map/pallas_call | solution.py:298
  59.9 0.6 %copy.9 = bf16[3,64,128]{2,1,0:T(8,128)(2,1)} copy(bf16[3,64,128]{2,1,0:T(8,128)(2,1)S(1)} %shard_map.73) | data formatting | bytes 98304

commit v5 on v4

--- a/solution.py
+++ b/solution.py
@@ -51,7 +51,7 @@
            gath, psend, precv, ins, rs, rr, ss, sr, lr, ps, pr):
     me, mm = lax.axis_index("dp"), lax.axis_index("mp")
     z, y = me // NY, me % NY
-    n_mp = precv.shape[1]
+    n_mp = precv.shape[0]
 
     def fwd(o):
         return ((z + o[0]) % NZ) * NY + (y + o[1]) % NY
@@ -152,8 +152,11 @@
                 row_copy(t, o).start()
 
     loads[2].wait()
-    for t, gs in ((0, groups[:4]), (1, groups[:4]), (0, groups[4:]), (1, groups[4:])):
-        for g in gs:
+    for g in groups[:4]:
+        serve(0, g)
+        serve(1, g)
+    for t in range(LAST):
+        for g in groups[4:]:
             serve(t, g)
     for dz in PLANES:
         serve(LAST, [(dz, dy) for dy in range(NY)])
@@ -268,27 +271,27 @@
         put(r, total[:, i * SEEDS:(i + 1) * SEEDS] / jnp.maximum(deg[i, 0:1, :], 1.0))
     put(RELS + LAST, total[:, 256:384])
 
-    def part_copy(a, d):
+    def part_copy(d):
         p = (mm + d) % n_mp
         return pltpu.make_async_remote_copy(
-            psend.at[a, p], precv.at[a, mm], ps.at[0], pr.at[a],
+            psend.at[p], precv.at[mm], ps.at[0], pr.at[0],
             device_id={"mp": p}, device_id_type=MESH)
 
     for a in range(TYPES):
         part = dot(wt[a], msgs[a]).astype(BF16)
         for p in range(n_mp):
-            psend[a, p] = part[p * 64:(p + 1) * 64]
-        for d in (4, 3, 5, 2, 6, 1, 7):
-            part_copy(a, d).start()
-        precv[a, mm] = psend[a, mm]
+            psend[p, a] = part[p * 64:(p + 1) * 64]
+    for d in (4, 3, 5, 2, 6, 1, 7):
+        part_copy(d).start()
+    precv[mm] = psend[mm]
     all_rows(LAST, sr.at[0]).wait_send()
+    many(psend.at[0:n_mp - 1], precv.at[0:n_mp - 1], ps.at[0], pr.at[0]).wait_recv()
     for a in range(TYPES):
-        many(psend.at[a, 0:n_mp - 1], precv.at[a, 0:n_mp - 1], ps.at[0], pr.at[a]).wait_recv()
-        typed = precv[a, 0].astype(F32)
+        typed = precv[0, a].astype(F32)
         for p in range(1, n_mp):
-            typed = typed + precv[a, p].astype(F32)
+            typed = typed + precv[p, a].astype(F32)
         out[a] = jnp.maximum(typed, 0.0).astype(BF16)
-    many(psend.at[:, 0:n_mp - 1], precv.at[:, 0:n_mp - 1], ps.at[0], pr.at[0]).wait_send()
+    many(psend.at[0:n_mp - 1], precv.at[0:n_mp - 1], ps.at[0], pr.at[0]).wait_send()
 
 
 def solution(mesh):
@@ -322,8 +325,8 @@
                 pltpu.VMEM((TYPES, 256, SEEDS), BF16),
                 pltpu.VMEM((TYPES, 512, 256), BF16),
                 pltpu.VMEM((64, 2048), BF16),
-                pltpu.VMEM((TYPES, n_mp, 64, SEEDS), BF16),
-                pltpu.VMEM((TYPES, n_mp, 64, SEEDS), BF16),
+                pltpu.VMEM((n_mp, TYPES, 64, SEEDS), BF16),
+                pltpu.VMEM((n_mp, TYPES, 64, SEEDS), BF16),
                 pltpu.SemaphoreType.DMA((7,)),
                 pltpu.SemaphoreType.DMA((1,)),
                 pltpu.SemaphoreType.DMA((8,)),
@@ -331,7 +334,7 @@
                 pltpu.SemaphoreType.DMA((LAST,)),
                 pltpu.SemaphoreType.DMA((NZ,)),
                 pltpu.SemaphoreType.DMA((1,)),
-                pltpu.SemaphoreType.DMA((TYPES,)),
+                pltpu.SemaphoreType.DMA((1,)),
             ],
             compiler_params=pltpu.CompilerParams(
                 collective_id=0, has_side_effects=True, vmem_limit_bytes=60000000),

time: 60.6 us -> 59.3 us (0.979)
  Pallas kernels: 59.8 us -> 58.5 us
    pallas_call x1, Pallas kernels: 59.8 us -> 58.5 us  [per_device(): pl.pallas_call(kernel, out_shape=pltpu.VMEM((TYPES, 64, SEEDS), BF16), in...]
where the time goes in v5:
time: 59.3 us; the launch traced here: 59.1 us
  Pallas kernels  58.5 us (99%)
  local copies, waits for them, and re-layouts  0.62 us (1%)
    pallas_call x1, Pallas kernels, per_device(): pl.pallas_call(kernel, out_shape=pltpu.VMEM((TYPES, 64, SEEDS), BF16), in...  58.5 us

profile of v5, /device:TPU:1, one launch (start us, length us, event | category | flops | bytes accessed | tf_op | source)
XLA Modules:
  0.0 59.1 jit_solution(8575615108222962626)
XLA Ops:
  0.0 58.5 %shard_map.73 = bf16[3,64,128]{2,1,0:T(8,128)(2,1)S(1)} custom-call(bf16[3,64,2048]{2,1,0:T(8,128)(2,1)} %feat_h.1, bf16[11,64,512]{2,1,0:T(8,128)(2,1)} %w_h.1, s32[3,1,2048]{2,1,0:T(1,128)} %bitcast.2, s32[3,2048]{1,0:T(4,128)} %row_h.1, s32[8,2048]{1,0:T(8,128)} %esrc_h.1, s32[8,2048]{1,0:T(8,128)} %edst_h.1, s32[1,8]{1,0:T(1,128)} %bitcast.3), custom_call_target="tpu_custom_call" | custom-call | tf_op jit(solution)/shard_map/pallas_call | solution.py:301
  58.5 0.6 %copy.9 = bf16[3,64,128]{2,1,0:T(8,128)(2,1)} copy(bf16[3,64,128]{2,1,0:T(8,128)(2,1)S(1)} %shard_map.73) | data formatting | bytes 98304

commit v6 on v5

--- a/solution.py
+++ b/solution.py
@@ -48,10 +48,15 @@
 def kernel(feat_h, w_h, own_h, row_h, esrc_h, edst_h, ecnt_h, out,
            feat, w, own, row, esrc, edst, ecnt,
            rq, req_out, req_in, send, recv, lk, pc, plo, lohot, counts, deg, msgs, wt,
-           gath, psend, precv, ins, rs, rr, ss, sr, lr, ps, pr):
+           gath, psend, precv, pair, comb, ins, rs, rr, ss, sr, lr, ps, pr):
     me, mm = lax.axis_index("dp"), lax.axis_index("mp")
     z, y = me // NY, me % NY
     n_mp = precv.shape[0]
+    nx = n_mp // 2
+    x, core = mm // 2, mm % 2
+    sibling = x * 2 + (1 - core)
+    opposite = ((x + 2) % nx) * 2 + core
+    beside = [((x + d) % nx) * 2 + k for d in (1, nx - 1) for k in range(2)]
 
     def fwd(o):
         return ((z + o[0]) % NZ) * NY + (y + o[1]) % NY
@@ -69,8 +74,8 @@
     barrier = pltpu.get_barrier_semaphore()
     for o in NEAREST[:0:-1]:
         pl.semaphore_signal(barrier, 1, device_id={"dp": fwd(o)}, device_id_type=MESH)
-    for d in range(1, n_mp):
-        pl.semaphore_signal(barrier, 1, device_id={"mp": (mm + d) % n_mp}, device_id_type=MESH)
+    for p in [opposite] + beside + [sibling]:
+        pl.semaphore_signal(barrier, 1, device_id={"mp": p}, device_id_type=MESH)
 
     loads = [
         pltpu.make_async_copy(src, dst, ins.at[i])
@@ -108,14 +113,14 @@
     for o in range(DP):
         req_out[o, :, :] = rq[pl.ds(o, TYPES, stride=DP), :]
 
-    pl.semaphore_wait(barrier, DP - 1 + n_mp - 1)
+    pl.semaphore_wait(barrier, DP - 1 + 6)
 
     def req_copy(o):
         return pltpu.make_async_remote_copy(
             req_out.at[fwd(o)], req_in.at[me], rs.at[0], rr.at[batch[o]],
             device_id={"dp": fwd(o)}, device_id_type=MESH)
 
-    for o in NEAREST[:0:-1]:
+    for o in NEAREST[1:]:
         req_copy(o).start()
     req_in[me] = req_out[me]
 
@@ -271,27 +276,38 @@
         put(r, total[:, i * SEEDS:(i + 1) * SEEDS] / jnp.maximum(deg[i, 0:1, :], 1.0))
     put(RELS + LAST, total[:, 256:384])
 
-    def part_copy(d):
-        p = (mm + d) % n_mp
+    def part_copy(p):
         return pltpu.make_async_remote_copy(
             psend.at[p], precv.at[mm], ps.at[0], pr.at[0],
             device_id={"mp": p}, device_id_type=MESH)
+
+    pair_copy = pltpu.make_async_remote_copy(
+        psend.at[((x + 2) % nx) * 2 + (1 - core)], pair, ps.at[1], pr.at[1],
+        device_id={"mp": sibling}, device_id_type=MESH)
+    far_copy = pltpu.make_async_remote_copy(
+        comb, precv.at[mm], ps.at[2], pr.at[2], device_id={"mp": opposite}, device_id_type=MESH)
 
     for a in range(TYPES):
         part = dot(wt[a], msgs[a]).astype(BF16)
         for p in range(n_mp):
             psend[p, a] = part[p * 64:(p + 1) * 64]
-    for d in (4, 3, 5, 2, 6, 1, 7):
-        part_copy(d).start()
-    precv[mm] = psend[mm]
+    pair_copy.start()
+    for p in beside:
+        part_copy(p).start()
+    part_copy(sibling).start()
+    pair_copy.wait_recv()
+    comb[...] = (psend[opposite].astype(F32) + pair[...].astype(F32)).astype(BF16)
+    far_copy.start()
     all_rows(LAST, sr.at[0]).wait_send()
-    many(psend.at[0:n_mp - 1], precv.at[0:n_mp - 1], ps.at[0], pr.at[0]).wait_recv()
-    for a in range(TYPES):
-        typed = precv[0, a].astype(F32)
-        for p in range(1, n_mp):
-            typed = typed + precv[p, a].astype(F32)
-        out[a] = jnp.maximum(typed, 0.0).astype(BF16)
-    many(psend.at[0:n_mp - 1], precv.at[0:n_mp - 1], ps.at[0], pr.at[0]).wait_send()
+    many(psend.at[0:5], precv.at[0:5], ps.at[0], pr.at[0]).wait_recv()
+    typed = psend[mm].astype(F32)
+    for p in beside + [sibling]:
+        typed = typed + precv[p].astype(F32)
+    far_copy.wait_recv()
+    out[...] = jnp.maximum(typed + precv[opposite].astype(F32), 0.0).astype(BF16)
+    many(psend.at[0:5], precv.at[0:5], ps.at[0], pr.at[0]).wait_send()
+    pair_copy.wait_send()
+    far_copy.wait_send()
 
 
 def solution(mesh):
@@ -327,14 +343,16 @@
                 pltpu.VMEM((64, 2048), BF16),
                 pltpu.VMEM((n_mp, TYPES, 64, SEEDS), BF16),
                 pltpu.VMEM((n_mp, TYPES, 64, SEEDS), BF16),
+                pltpu.VMEM((TYPES, 64, SEEDS), BF16),
+                pltpu.VMEM((TYPES, 64, SEEDS), BF16),
                 pltpu.SemaphoreType.DMA((7,)),
                 pltpu.SemaphoreType.DMA((1,)),
                 pltpu.SemaphoreType.DMA((8,)),
                 pltpu.SemaphoreType.DMA((TYPES,)),
                 pltpu.SemaphoreType.DMA((LAST,)),
                 pltpu.SemaphoreType.DMA((NZ,)),
-                pltpu.SemaphoreType.DMA((1,)),
-                pltpu.SemaphoreType.DMA((1,)),
+                pltpu.SemaphoreType.DMA((3,)),
+                pltpu.SemaphoreType.DMA((3,)),
             ],
             compiler_params=pltpu.CompilerParams(
                 collective_id=0, has_side_effects=True, vmem_limit_bytes=60000000),

time: 59.3 us -> 60.1 us (1.013)
  Pallas kernels: 58.5 us -> 59.4 us
    pallas_call x1, Pallas kernels: 58.5 us -> 59.4 us  [per_device(): pl.pallas_call(kernel, out_shape=pltpu.VMEM((TYPES, 64, SEEDS), BF16), in...]
where the time goes in v6:
time: 60.1 us; the launch traced here: 60 us
  Pallas kernels  59.4 us (99%)
  local copies, waits for them, and re-layouts  0.62 us (1%)
    pallas_call x1, Pallas kernels, per_device(): pl.pallas_call(kernel, out_shape=pltpu.VMEM((TYPES, 64, SEEDS), BF16), in...  59.4 us

profile of v6, /device:TPU:1, one launch (start us, length us, event | category | flops | bytes accessed | tf_op | source)
XLA Modules:
  0.0 60.0 jit_solution(10855883894209867310)
XLA Ops:
  0.0 59.4 %shard_map.73 = bf16[3,64,128]{2,1,0:T(8,128)(2,1)S(1)} custom-call(bf16[3,64,2048]{2,1,0:T(8,128)(2,1)} %feat_h.1, bf16[11,64,512]{2,1,0:T(8,128)(2,1)} %w_h.1, s32[3,1,2048]{2,1,0:T(1,128)} %bitcast.2, s32[3,2048]{1,0:T(4,128)} %row_h.1, s32[8,2048]{1,0:T(8,128)} %esrc_h.1, s32[8,2048]{1,0:T(8,128)} %edst_h.1, s32[1,8]{1,0:T(1,128)} %bitcast.3), custom_call_target="tpu_custom_call" | custom-call | tf_op jit(solution)/shard_map/pallas_call | solution.py:317
  59.4 0.6 %copy.9 = bf16[3,64,128]{2,1,0:T(8,128)(2,1)} copy(bf16[3,64,128]{2,1,0:T(8,128)(2,1)S(1)} %shard_map.73) | data formatting | bytes 98304

commit v7 on v5

--- a/solution.py
+++ b/solution.py
@@ -152,12 +152,9 @@
                 row_copy(t, o).start()
 
     loads[2].wait()
-    for g in groups[:4]:
+    for g in groups:
         serve(0, g)
         serve(1, g)
-    for t in range(LAST):
-        for g in groups[4:]:
-            serve(t, g)
     for dz in PLANES:
         serve(LAST, [(dz, dy) for dy in range(NY)])
 

time: 59.3 us -> 65.2 us (1.099)
  the two profiles are of different devices: /device:TPU:1 before, /device:TPU:64 now
where the time goes in v7:
time: 65.2 us; the launch traced here: 65.1 us
  Pallas kernels  64.4 us (99%)
    pallas_call x1, Pallas kernels, per_device(): pl.pallas_call(kernel, out_shape=pltpu.VMEM((TYPES, 64, SEEDS), BF16), in...  64.4 us

profile of v7, /device:TPU:64, one launch (start us, length us, event | category | flops | bytes accessed | tf_op | source)
XLA Modules:
  0.0 65.1 jit_solution(16863369318906405329)
XLA Ops:
  0.0 64.4 %shard_map.73 = bf16[3,64,128]{2,1,0:T(8,128)(2,1)S(1)} custom-call(bf16[3,64,2048]{2,1,0:T(8,128)(2,1)} %feat_h.1, bf16[11,64,512]{2,1,0:T(8,128)(2,1)} %w_h.1, s32[3,1,2048]{2,1,0:T(1,128)} %bitcast.2, s32[3,2048]{1,0:T(4,128)} %row_h.1, s32[8,2048]{1,0:T(8,128)} %esrc_h.1, s32[8,2048]{1,0:T(8,128)} %edst_h.1, s32[1,8]{1,0:T(1,128)} %bitcast.3), custom_call_target="tpu_custom_call" | custom-call | tf_op jit(solution)/shard_map/pallas_call | solution.py:298
  64.4 0.6 copy.9
